TPU v7x, 512 devices: a 8x2x16 block of a 8x8x16 slice. The times are simulated.
512 devices in a mesh: runs: 2 (over y), gx: 16 (over z), gy: 8 (over x), gz: 2 (over core).
Axes of the slice: x: 8, y: 2, z: 16, core: 2. Of those that a mesh axis runs over, the one named last changes fastest.
The devices are a block of a 8x8x16 slice.
Arguments:
- positions: float32 [3, 8, 65536], P(None, None, ('runs', 'gx', 'gy', 'gz')), parts along dimension 2, as said below
- velocities: float32 [3, 8, 65536], P(None, None, ('runs', 'gx', 'gy', 'gz')), parts along dimension 2, may hold values from -5 to 5
- send_list: int32 [91136], P(('runs', 'gx', 'gy', 'gz')), parts along dimension 0, may hold values from 0 to 127
- pair_list: int32 [2, 917504], P(None, ('runs', 'gx', 'gy', 'gz')), parts along dimension 1, may hold values from 0 to 306, as said below
- constraint_flags: int32 [7, 65536], P(None, ('runs', 'gx', 'gy', 'gz')), parts along dimension 1, may hold values 0 or 1
Outputs:
- final_positions: float32 [3, 8, 65536], P(None, None, ('runs', 'gx', 'gy', 'gz')), parts along dimension 2
- final_velocities: float32 [3, 8, 65536], P(None, None, ('runs', 'gx', 'gy', 'gz')), parts along dimension 2
- energies: float32 [6, 2], P('runs'), parts along dimension 0
There are 2 independent parts, one for each index of `runs`. A program takes and returns all parts, laid end to end along the dimension named above; each array names one. Nothing has to cross between parts.
Inputs may be any that keep to these rules, and one draw needn't show every extreme that they name: `pair_list`: each domain's 1792 slots name clusters of its extended set: 0 to 127 its own, then its received zone blocks in order; padding slots hold 306 in both rows; every cluster appears in a slot with itself; no unordered pair appears twice. `positions`: eight beads of a cluster lie in its cell of side 1, the cells of a domain filling a box of 1 by 8 by 16; neighbouring beads of a cluster are between 0.25 and 0.6 apart.
All inputs are finite; a program needn't handle non-finite values. No bound on the sum of `constraint_flags` on one device may be relied on, other than what follows from the above.
Results may differ from a plain program's by a relative error of at most 0.0003.
Values sent between devices are 32-bit elements; how exact they have to be, the bound alone decides.
A program may use at most 64 MiB of HBM per device.

v0:
```python
import jax
import jax.numpy as jnp
import numpy as np
from jax import lax
from jax.sharding import PartitionSpec as P

CX = 1
CY = 8
CZ = 16
ITERS = 3
NORDER = 4


time_step = 0.02
strength = 2.0
root_half = 0.7071067811865476
zone_list = ((1, 0, 0), (0, 1, 0), (0, 0, 1), (1, 1, 0), (1, 0, 1), (0, 1, 1), (1, 1, 1))


def from_behind(value, axis, by):
    count = lax.axis_size(axis)
    return lax.ppermute(value, axis, [(i, (i + by) % count) for i in range(count)])


def over_axes(value, axes):
    for axis in axes:
        value = lax.psum(value, axis)
    return value


def zone_sizes():
    return tuple(
        (
            (CX if direction[0] == 0 else 1)
            * (CY if direction[1] == 0 else 1)
            * (CZ if direction[2] == 0 else 1)
            for direction in zone_list
        )
    )


def split_blocks(packed, block_sizes):
    pieces = []
    position = 0
    for length in block_sizes:
        pieces.append(packed[:, :, position : position + length])
        position += length
    return pieces


def shell_offsets():
    block_sizes = zone_sizes()
    columns = []
    for number in range(7):
        direction = zone_list[number]
        column = np.array(
            [[direction[0] * CX], [direction[1] * CY], [direction[2] * CZ]], np.float32
        )
        columns.append(np.tile(column, (1, block_sizes[number])))
    return jnp.asarray(np.concatenate(columns, axis=1))[:, None, :]


def share_coords(coords, send_list):
    sizes_all = zone_sizes()
    outgoing = split_blocks(jnp.take(coords, send_list, axis=2), sizes_all)
    along_y = from_behind(
        jnp.concatenate([outgoing[1], outgoing[3], outgoing[5], outgoing[6]], axis=2), "gy", -1
    )
    got_y = split_blocks(along_y, [sizes_all[1], sizes_all[3], sizes_all[5], sizes_all[6]])
    along_x = from_behind(
        jnp.concatenate([outgoing[0], outgoing[4], got_y[1], got_y[3]], axis=2), "gx", -1
    )
    got_x = split_blocks(along_x, [sizes_all[0], sizes_all[4], sizes_all[3], sizes_all[6]])
    along_z = from_behind(
        jnp.concatenate([outgoing[2], got_x[1], got_y[2], got_x[3]], axis=2), "gz", -1
    )
    got_z = split_blocks(along_z, [sizes_all[2], sizes_all[4], sizes_all[5], sizes_all[6]])
    received = [got_x[0], got_y[0], got_z[0], got_x[2], got_z[1], got_z[2], got_z[3]]
    return jnp.concatenate(received, axis=2) + shell_offsets()


def return_forces(halo_forces):
    sizes_all = zone_sizes()
    outgoing = split_blocks(halo_forces, sizes_all)
    along_z = from_behind(
        jnp.concatenate([outgoing[2], outgoing[4], outgoing[5], outgoing[6]], axis=2), "gz", 1
    )
    got_z = split_blocks(along_z, [sizes_all[2], sizes_all[4], sizes_all[5], sizes_all[6]])
    along_x = from_behind(
        jnp.concatenate([outgoing[0], outgoing[3], got_z[1], got_z[3]], axis=2), "gx", 1
    )
    got_x = split_blocks(along_x, [sizes_all[0], sizes_all[3], sizes_all[4], sizes_all[6]])
    settled = [got_x[0], got_z[0], got_x[2]]
    pending = [got_x[1], got_z[2], got_x[3]]
    along_y = from_behind(
        jnp.concatenate([outgoing[1], pending[0], pending[1], pending[2]], axis=2), "gy", 1
    )
    got_y = split_blocks(along_y, [sizes_all[1], sizes_all[3], sizes_all[5], sizes_all[6]])
    return jnp.concatenate(
        [settled[0], got_y[0], settled[1], got_y[1], settled[2], got_y[2], got_y[3]], axis=2
    )


def pair_tables(pair_list, extended_count):
    rows = lax.broadcasted_iota(jnp.int32, (extended_count, pair_list.shape[1]), 0)
    first_table = (rows == pair_list[0][None, :]).astype(jnp.float32)
    second_table = (rows == pair_list[1][None, :]).astype(jnp.float32)
    return (first_table, second_table)


def domain_forces(extended, pair_list, tables):
    extended_count = extended.shape[2]
    slot_count = pair_list.shape[1]
    first_ids = pair_list[0]
    second_ids = pair_list[1]
    flat = extended.reshape(24, extended_count)
    first_coords = jnp.dot(flat, tables[0], precision=lax.Precision.HIGHEST).reshape(
        3, 8, slot_count
    )
    second_coords = jnp.dot(flat, tables[1], precision=lax.Precision.HIGHEST).reshape(
        3, 8, slot_count
    )
    separation = first_coords[:, :, None, :] - second_coords[:, None, :, :]
    scaled = jnp.sum(separation * separation, axis=0)
    intersect = jnp.maximum(1.0 - scaled, 0.0)
    bead_row = lax.broadcasted_iota(jnp.int32, (8, 8, 1), 0)
    bead_column = lax.broadcasted_iota(jnp.int32, (8, 8, 1), 1)
    self_pair = (first_ids == second_ids)[None, None, :]
    usable = (first_ids < extended_count - 1)[None, None, :]
    weight = (jnp.where(self_pair, bead_row < bead_column, True) & usable).astype(jnp.float32)
    energy = strength * jnp.sum(weight * intersect * intersect * intersect)
    magnitude = 6.0 * strength * weight * intersect * intersect
    pushing = magnitude[None] * separation
    on_first = jnp.sum(pushing, axis=2).reshape(24, slot_count)
    on_second = (-jnp.sum(pushing, axis=1)).reshape(24, slot_count)
    contract = (((1,), (1,)), ((), ()))
    forces = lax.dot_general(on_first, tables[0], contract, precision=lax.Precision.HIGHEST)
    forces = forces + lax.dot_general(
        on_second, tables[1], contract, precision=lax.Precision.HIGHEST
    )
    return (forces.reshape(3, 8, extended_count), energy)


def local_forces(coords, send_list, pair_list, tables):
    halo_coords = share_coords(coords, send_list)
    dummy_cluster = jnp.zeros((3, 8, 1), jnp.float32)
    extended = jnp.concatenate([coords, halo_coords, dummy_cluster], axis=2)
    forces, energy = domain_forces(extended, pair_list, tables)
    cluster_count = coords.shape[2]
    returned = return_forces(forces[:, :, cluster_count : cluster_count + send_list.shape[0]])
    home_forces = forces[:, :, :cluster_count].at[:, :, send_list].add(returned)
    return (home_forces, energy)


def link_vectors(coords):
    return coords[:, :-1, :] - coords[:, 1:, :]


def link_lengths(coords):
    vectors = link_vectors(coords)
    return jnp.sqrt(jnp.sum(vectors * vectors, axis=0))


def expand(coupling, source):
    coupling_down = jnp.pad(coupling, ((1, 0), (0, 0)))
    coupling_up = jnp.pad(coupling, ((0, 1), (0, 0)))
    series = source
    result = source
    for expansion in range(NORDER):
        series = (
            coupling_down * jnp.pad(series, ((1, 0), (0, 0)))[:-1]
            + coupling_up * jnp.pad(series, ((0, 1), (0, 0)))[1:]
        )
        result = result + series
    return result


def apply_links(coords, directions, solution):
    shifts = directions * (root_half * solution)[None]
    return (
        coords
        - jnp.pad(shifts, ((0, 0), (0, 1), (0, 0)))
        + jnp.pad(shifts, ((0, 0), (1, 0), (0, 0)))
    )


def constrain(previous, updated, rest_length, link_flags):
    old_vectors = link_vectors(previous)
    directions = (
        old_vectors / jnp.maximum(jnp.sqrt(jnp.sum(old_vectors * old_vectors, axis=0)), 0.2)[None]
    )
    coupling = (
        0.5
        * jnp.sum(directions[:, :-1] * directions[:, 1:], axis=0)
        * link_flags[:-1]
        * link_flags[1:]
    )
    projected = jnp.sum(directions * link_vectors(updated), axis=0)
    solution = expand(coupling, link_flags * root_half * (projected - rest_length))
    updated = apply_links(updated, directions, solution)
    vectors = link_vectors(updated)
    squared = jnp.sum(vectors * vectors, axis=0)
    target = jnp.sqrt(
        jnp.maximum(2.0 * rest_length * rest_length - squared, 0.25 * rest_length * rest_length)
    )
    solution = expand(coupling, link_flags * root_half * (rest_length - target))
    updated = apply_links(updated, directions, solution)
    return updated


def on_device(positions, velocities, send_list, pair_list, constraint_flags):
    link_flags = constraint_flags.astype(jnp.float32)
    rest_length = link_lengths(positions)
    bead_total = 8 * positions.shape[2] * lax.axis_size(("gx", "gy", "gz"))
    tables = pair_tables(pair_list, positions.shape[2] + send_list.shape[0] + 1)
    forces, potential = local_forces(positions, send_list, pair_list, tables)
    energy_rows = []
    for iteration in range(ITERS):
        half_speed = velocities + 0.5 * time_step * forces
        updated = constrain(positions, positions + time_step * half_speed, rest_length, link_flags)
        half_speed = (updated - positions) / time_step
        forces, potential = local_forces(updated, send_list, pair_list, tables)
        velocities = half_speed + 0.5 * time_step * forces
        positions = updated
        kinetic = 0.5 * jnp.sum(velocities * velocities)
        energy_rows.append(jnp.stack([potential, kinetic]))
    energies = jnp.stack(energy_rows)
    energies = over_axes(energies, ("gx", "gy", "gz"))
    return (positions, velocities, energies / bead_total)


def solution(mesh):
    return jax.shard_map(
        on_device,
        mesh=mesh,
        in_specs=(
            P(None, None, ("runs", "gx", "gy", "gz")),
            P(None, None, ("runs", "gx", "gy", "gz")),
            P(("runs", "gx", "gy", "gz")),
            P(None, ("runs", "gx", "gy", "gz")),
            P(None, ("runs", "gx", "gy", "gz")),
        ),
        out_specs=(
            P(None, None, ("runs", "gx", "gy", "gz")),
            P(None, None, ("runs", "gx", "gy", "gz")),
            P("runs", None),
        ),
        check_vma=False,
    )
```

profile of v0, /device:TPU:65, one launch (start us, length us, event | category | flops | bytes accessed | tf_op | source)
XLA Modules:
  0.0 284.2 jit_solution(5822474635701368043)
XLA Ops:
  4.1 6.3 %collective-permute-start = (f32[3,8,34]{2,1,0:T(8,128)S(1)}, f32[3,8,34]{2,1,0:T(8,128)S(1)}, u32[]{:S(2)}, u32[]{:S(2)}) collective-permute-start(f32[3,8,34]{2,1,0:T(8,128)S(1)} %pad_maximum_fusion.8), channel_id=1, source_target_pairs={{0,14},{2,0},{4,2},{6,4},{8,6},{10,8},{12,10},{14,12},{1,15},{3,1}... | collective-permute-start | bytes 9800 | tf_op jit(solution)/shard_map/ppermute | solution.py:22
  11.5 43.7 %collective-permute-start.1 = (f32[3,8,153]{2,1,0:T(8,128)S(1)}, f32[3,8,153]{2,1,0:T(8,128)S(1)}, u32[]{:S(2)}, u32[]{:S(2)}) collective-permute-start(f32[3,8,153]{2,1,0:T(8,128)S(1)} %pad_maximum_fusion), channel_id=1, source_target_pairs={{0,240},{16,0},{32,16},{48,32},{64,48},{80,64},{96,80},{112,96},{1... | collective-permute-start | bytes 44072 | tf_op jit(solution)/shard_map/ppermute | solution.py:22
  55.2 0.9 collective-permute-done.1
  56.3 4.2 %collective-permute-start.2 = (f32[3,8,18]{2,1,0:T(8,128)S(1)}, f32[3,8,18]{2,1,0:T(8,128)S(1)}, u32[]{:S(2)}, u32[]{:S(2)}) collective-permute-start(f32[3,8,18]{2,1,0:T(8,128)S(1)} %pad_maximum_fusion.9), channel_id=1, source_target_pairs={{0,1},{1,0},{2,3},{3,2},{4,5},{5,4},{6,7},{7,6},{8,9},{9,8},{10,11... | collective-permute-start | bytes 5192 | tf_op jit(solution)/shard_map/ppermute | solution.py:22
  61.5 0.9 fusion.24
  62.4 0.9 fusion.11
  64.1 1.1 fusion.3
  65.2 1.1 fusion.55
  66.6 2.3 collective-permute-start.3
  69.9 1.9 collective-permute-start.4
  71.9 4.4 %collective-permute-done.4 = f32[3,8,153]{2,1,0:T(8,128)S(1)} collective-permute-done((f32[3,8,153]{2,1,0:T(8,128)S(1)}, f32[3,8,153]{2,1,0:T(8,128)S(1)}, u32[]{:S(2)}, u32[]{:S(2)}) %collective-permute-start.4) | collective-permute-done | bytes 14720 | tf_op jit(solution)/shard_map/ppermute | solution.py:22
  76.5 1.9 collective-permute-start.5
  78.7 4.0 %collective-permute-done.5 = f32[3,8,34]{2,1,0:T(8,128)S(1)} collective-permute-done((f32[3,8,34]{2,1,0:T(8,128)S(1)}, f32[3,8,34]{2,1,0:T(8,128)S(1)}, u32[]{:S(2)}, u32[]{:S(2)}) %collective-permute-start.5) | collective-permute-done | bytes 3296 | tf_op jit(solution)/shard_map/ppermute | solution.py:22
  83.2 7.2 %scatter_fusion = f32[3,8,128]{1,0,2:T(4,128)S(1)} fusion(f32[3,8,128]{1,0,2:T(4,128)S(1)} %copy.120, s32[178]{0:T(256)S(1)} %compare_select_fusion, f32[178,3,8]{2,1,0:T(4,128)S(1)} %copy.102), kind=kCustom, calls=%fused_computation.4 | custom fusion | flops 4272 | bytes 51976 | tf_op jit(solution)/shard_map/scatter-add | solution.py:151
  92.1 3.4 %collective-permute-start.6 = (f32[3,8,34]{2,1,0:T(8,128)S(1)}, f32[3,8,34]{2,1,0:T(8,128)S(1)}, u32[]{:S(2)}, u32[]{:S(2)}) collective-permute-start(f32[3,8,34]{2,1,0:T(8,128)S(1)} %pad_maximum_fusion.12), channel_id=1, source_target_pairs={{0,14},{2,0},{4,2},{6,4},{8,6},{10,8},{12,10},{14,12},{1,15},{3,1}... | collective-permute-start | bytes 9800 | tf_op jit(solution)/shard_map/ppermute | solution.py:22
  95.6 1.0 collective-permute-done.6
  96.8 3.4 %collective-permute-start.7 = (f32[3,8,153]{2,1,0:T(8,128)S(1)}, f32[3,8,153]{2,1,0:T(8,128)S(1)}, u32[]{:S(2)}, u32[]{:S(2)}) collective-permute-start(f32[3,8,153]{2,1,0:T(8,128)S(1)} %pad_maximum_fusion.2), channel_id=1, source_target_pairs={{0,240},{16,0},{32,16},{48,32},{64,48},{80,64},{96,80},{112,96},{1... | collective-permute-start | bytes 44072 | tf_op jit(solution)/shard_map/ppermute | solution.py:22
  100.2 1.2 collective-permute-done.7
  101.6 6.3 %collective-permute-start.8 = (f32[3,8,18]{2,1,0:T(8,128)S(1)}, f32[3,8,18]{2,1,0:T(8,128)S(1)}, u32[]{:S(2)}, u32[]{:S(2)}) collective-permute-start(f32[3,8,18]{2,1,0:T(8,128)S(1)} %pad_maximum_fusion.13), channel_id=1, source_target_pairs={{0,1},{1,0},{2,3},{3,2},{4,5},{5,4},{6,7},{7,6},{8,9},{9,8},{10,11... | collective-permute-start | bytes 5192 | tf_op jit(solution)/shard_map/ppermute | solution.py:22
  108.9 0.9 fusion.22
  109.8 0.9 fusion.9
  111.4 1.1 fusion.1
  112.5 1.1 fusion.59
  113.9 2.3 collective-permute-start.9
  117.2 1.9 collective-permute-start.10
  119.2 4.1 %collective-permute-done.10 = f32[3,8,153]{2,1,0:T(8,128)S(1)} collective-permute-done((f32[3,8,153]{2,1,0:T(8,128)S(1)}, f32[3,8,153]{2,1,0:T(8,128)S(1)}, u32[]{:S(2)}, u32[]{:S(2)}) %collective-permute-start.10) | collective-permute-done | bytes 14720 | tf_op jit(solution)/shard_map/ppermute | solution.py:22
  123.5 2.1 collective-permute-start.11
  125.9 3.6 %collective-permute-done.11 = f32[3,8,34]{2,1,0:T(8,128)S(1)} collective-permute-done((f32[3,8,34]{2,1,0:T(8,128)S(1)}, f32[3,8,34]{2,1,0:T(8,128)S(1)}, u32[]{:S(2)}, u32[]{:S(2)}) %collective-permute-start.11) | collective-permute-done | bytes 3296 | tf_op jit(solution)/shard_map/ppermute | solution.py:22
  129.9 7.2 %scatter_fusion.1 = f32[3,8,128]{1,0,2:T(4,128)S(1)} fusion(f32[3,8,128]{1,0,2:T(4,128)S(1)} %copy.121, s32[178]{0:T(256)S(1)} %compare_select_fusion, f32[178,3,8]{2,1,0:T(4,128)S(1)} %copy.107), kind=kCustom, calls=%fused_computation.5 | custom fusion | flops 4272 | bytes 51976 | tf_op jit(solution)/shard_map/scatter-add | solution.py:151
  138.9 3.4 %collective-permute-start.12 = (f32[3,8,34]{2,1,0:T(8,128)S(1)}, f32[3,8,34]{2,1,0:T(8,128)S(1)}, u32[]{:S(2)}, u32[]{:S(2)}) collective-permute-start(f32[3,8,34]{2,1,0:T(8,128)S(1)} %pad_maximum_fusion.16), channel_id=1, source_target_pairs={{0,14},{2,0},{4,2},{6,4},{8,6},{10,8},{12,10},{14,12},{1,15},{3,1}... | collective-permute-start | bytes 9800 | tf_op jit(solution)/shard_map/ppermute | solution.py:22
  142.3 1.0 collective-permute-done.12
  143.6 3.4 %collective-permute-start.13 = (f32[3,8,153]{2,1,0:T(8,128)S(1)}, f32[3,8,153]{2,1,0:T(8,128)S(1)}, u32[]{:S(2)}, u32[]{:S(2)}) collective-permute-start(f32[3,8,153]{2,1,0:T(8,128)S(1)} %pad_maximum_fusion.4), channel_id=1, source_target_pairs={{0,240},{16,0},{32,16},{48,32},{64,48},{80,64},{96,80},{112,96},{1... | collective-permute-start | bytes 44072 | tf_op jit(solution)/shard_map/ppermute | solution.py:22
  147.0 1.2 collective-permute-done.13
  148.3 6.3 %collective-permute-start.14 = (f32[3,8,18]{2,1,0:T(8,128)S(1)}, f32[3,8,18]{2,1,0:T(8,128)S(1)}, u32[]{:S(2)}, u32[]{:S(2)}) collective-permute-start(f32[3,8,18]{2,1,0:T(8,128)S(1)} %pad_maximum_fusion.17), channel_id=1, source_target_pairs={{0,1},{1,0},{2,3},{3,2},{4,5},{5,4},{6,7},{7,6},{8,9},{9,8},{10,11... | collective-permute-start | bytes 5192 | tf_op jit(solution)/shard_map/ppermute | solution.py:22
  155.6 0.9 fusion.20
  156.5 0.9 fusion.7
  158.2 1.1 fusion
  159.3 1.1 fusion.61
  160.7 2.3 collective-permute-start.15
  164.0 1.9 collective-permute-start.16
  165.9 4.1 %collective-permute-done.16 = f32[3,8,153]{2,1,0:T(8,128)S(1)} collective-permute-done((f32[3,8,153]{2,1,0:T(8,128)S(1)}, f32[3,8,153]{2,1,0:T(8,128)S(1)}, u32[]{:S(2)}, u32[]{:S(2)}) %collective-permute-start.16) | collective-permute-done | bytes 14720 | tf_op jit(solution)/shard_map/ppermute | solution.py:22
  170.2 1.9 collective-permute-start.17
  172.4 3.7 %collective-permute-done.17 = f32[3,8,34]{2,1,0:T(8,128)S(1)} collective-permute-done((f32[3,8,34]{2,1,0:T(8,128)S(1)}, f32[3,8,34]{2,1,0:T(8,128)S(1)}, u32[]{:S(2)}, u32[]{:S(2)}) %collective-permute-start.17) | collective-permute-done | bytes 3296 | tf_op jit(solution)/shard_map/ppermute | solution.py:22
  176.6 7.2 %scatter_fusion.2 = f32[3,8,128]{1,0,2:T(4,128)S(1)} fusion(f32[3,8,128]{1,0,2:T(4,128)S(1)} %copy.122, s32[178]{0:T(256)S(1)} %compare_select_fusion, f32[178,3,8]{2,1,0:T(4,128)S(1)} %copy.112), kind=kCustom, calls=%fused_computation.6 | custom fusion | flops 4272 | bytes 51976 | tf_op jit(solution)/shard_map/scatter-add | solution.py:151
  186.2 3.4 %collective-permute-start.18 = (f32[3,8,34]{2,1,0:T(8,128)S(1)}, f32[3,8,34]{2,1,0:T(8,128)S(1)}, u32[]{:S(2)}, u32[]{:S(2)}) collective-permute-start(f32[3,8,34]{2,1,0:T(8,128)S(1)} %pad_maximum_fusion.20), channel_id=1, source_target_pairs={{0,14},{2,0},{4,2},{6,4},{8,6},{10,8},{12,10},{14,12},{1,15},{3,1}... | collective-permute-start | bytes 9800 | tf_op jit(solution)/shard_map/ppermute | solution.py:22
  189.7 1.0 collective-permute-done.18
  190.9 3.4 %collective-permute-start.19 = (f32[3,8,153]{2,1,0:T(8,128)S(1)}, f32[3,8,153]{2,1,0:T(8,128)S(1)}, u32[]{:S(2)}, u32[]{:S(2)}) collective-permute-start(f32[3,8,153]{2,1,0:T(8,128)S(1)} %pad_maximum_fusion.6), channel_id=1, source_target_pairs={{0,240},{16,0},{32,16},{48,32},{64,48},{80,64},{96,80},{112,96},{1... | collective-permute-start | bytes 44072 | tf_op jit(solution)/shard_map/ppermute | solution.py:22
  194.3 1.2 collective-permute-done.19
  195.7 6.5 %collective-permute-start.20 = (f32[3,8,18]{2,1,0:T(8,128)S(1)}, f32[3,8,18]{2,1,0:T(8,128)S(1)}, u32[]{:S(2)}, u32[]{:S(2)}) collective-permute-start(f32[3,8,18]{2,1,0:T(8,128)S(1)} %pad_maximum_fusion.21), channel_id=1, source_target_pairs={{0,1},{1,0},{2,3},{3,2},{4,5},{5,4},{6,7},{7,6},{8,9},{9,8},{10,11... | collective-permute-start | bytes 5192 | tf_op jit(solution)/shard_map/ppermute | solution.py:22
  203.0 0.9 fusion.18
  203.8 0.9 fusion.5
  204.9 1.1 fusion.66
  206.4 1.1 fusion.2
  207.5 1.1 fusion.57
  208.9 2.3 collective-permute-start.21
  212.2 1.9 collective-permute-start.22
  216.7 1.6 collective-permute-done.22
  218.4 1.9 collective-permute-start.23
  221.4 3.0 %collective-permute-done.23 = f32[3,8,34]{2,1,0:T(8,128)S(1)} collective-permute-done((f32[3,8,34]{2,1,0:T(8,128)S(1)}, f32[3,8,34]{2,1,0:T(8,128)S(1)}, u32[]{:S(2)}, u32[]{:S(2)}) %collective-permute-start.23) | collective-permute-done | bytes 3296 | tf_op jit(solution)/shard_map/ppermute | solution.py:22
  224.9 7.2 %scatter_fusion.3 = f32[3,8,128]{1,0,2:T(4,128)S(1)} fusion(f32[3,8,128]{1,0,2:T(4,128)S(1)} %copy.123, s32[178]{0:T(256)S(1)} %compare_select_fusion, f32[178,3,8]{2,1,0:T(4,128)S(1)} %copy.117), kind=kCustom, calls=%fused_computation.7 | custom fusion | flops 4272 | bytes 51976 | tf_op jit(solution)/shard_map/scatter-add | solution.py:151
  232.1 1.2 multiply_reduce_fusion
  234.1 21.7 %psum.21 = f32[3,2]{1,0:T(4,128)S(1)} all-reduce(f32[3,2]{1,0:T(4,128)S(1)} %pad_maximum_fusion.24), channel_id=1, replica_groups=mesh['runs'=2,'gx'=16,'gy'=8,'gz'=2] {'gx'}, use_global_device_ids=true, to_apply=%region_34.36 | all-reduce | flops 6 | bytes 48 | tf_op jit(solution)/shard_map/psum | solution.py:27
  255.8 11.9 %psum.22 = f32[3,2]{1,0:T(4,128)S(1)} all-reduce(f32[3,2]{1,0:T(4,128)S(1)} %psum.21), channel_id=1, replica_groups=mesh['runs'=2,'gx'=16,'gy'=8,'gz'=2] {'gy'}, use_global_device_ids=true, to_apply=%region_35.37 | all-reduce | flops 6 | bytes 48 | tf_op jit(solution)/shard_map/psum | solution.py:27
  267.8 15.8 %psum.23 = f32[3,2]{1,0:T(4,128)S(1)} all-reduce(f32[3,2]{1,0:T(4,128)S(1)} %psum.22), channel_id=1, replica_groups=mesh['runs'=2,'gx'=16,'gy'=8,'gz'=2] {'gz'}, use_global_device_ids=true, to_apply=%region_36.38 | all-reduce | flops 6 | bytes 48 | tf_op jit(solution)/shard_map/psum | solution.py:27
  (264 shorter events, 27.9 us)
Async XLA Ops:
  2.0 8.5 %copy-start.4 = (s32[2,1792]{1,0:T(2,128)S(1)}, s32[2,1792]{1,0:T(2,128)}, u32[]{:S(2)}) copy-start(s32[2,1792]{1,0:T(2,128)} %param.14) | copy-start | bytes 43012
  3.9 57.6 %copy-start.3 = (f32[3,178]{1,0:T(4,128)S(1)}, f32[3,178]{1,0:T(4,128)}, u32[]{:S(2)}) copy-start(f32[3,178]{1,0:T(4,128)} %constant.57.clone) | copy-start | bytes 6412
  3.9 57.7 %copy-start = (f32[3,8,128]{2,1,0:T(8,128)S(1)}, f32[3,8,128]{2,1,0:T(8,128)}, u32[]{:S(2)}) copy-start(f32[3,8,128]{2,1,0:T(8,128)} %param.11) | copy-start | bytes 36868
  4.1 7.1 %collective-permute-start = (f32[3,8,34]{2,1,0:T(8,128)S(1)}, f32[3,8,34]{2,1,0:T(8,128)S(1)}, u32[]{:S(2)}, u32[]{:S(2)}) collective-permute-start(f32[3,8,34]{2,1,0:T(8,128)S(1)} %pad_maximum_fusion.8), channel_id=1, source_target_pairs={{0,14},{2,0},{4,2},{6,4},{8,6},{10,8},{12,10},{14,12},{1,15},{3,1}... | collective-permute-start | bytes 9800 | tf_op jit(solution)/shard_map/ppermute | solution.py:22
  11.5 44.7 %collective-permute-start.1 = (f32[3,8,153]{2,1,0:T(8,128)S(1)}, f32[3,8,153]{2,1,0:T(8,128)S(1)}, u32[]{:S(2)}, u32[]{:S(2)}) collective-permute-start(f32[3,8,153]{2,1,0:T(8,128)S(1)} %pad_maximum_fusion), channel_id=1, source_target_pairs={{0,240},{16,0},{32,16},{48,32},{64,48},{80,64},{96,80},{112,96},{1... | collective-permute-start | bytes 44072 | tf_op jit(solution)/shard_map/ppermute | solution.py:22
  56.3 5.1 %collective-permute-start.2 = (f32[3,8,18]{2,1,0:T(8,128)S(1)}, f32[3,8,18]{2,1,0:T(8,128)S(1)}, u32[]{:S(2)}, u32[]{:S(2)}) collective-permute-start(f32[3,8,18]{2,1,0:T(8,128)S(1)} %pad_maximum_fusion.9), channel_id=1, source_target_pairs={{0,1},{1,0},{2,3},{3,2},{4,5},{5,4},{6,7},{7,6},{8,9},{9,8},{10,11... | collective-permute-start | bytes 5192 | tf_op jit(solution)/shard_map/ppermute | solution.py:22
  65.2 13.2 %copy-start.1 = (s32[7,128]{1,0:T(8,128)S(1)}, s32[7,128]{1,0:T(8,128)}, u32[]{:S(2)}) copy-start(s32[7,128]{1,0:T(8,128)} %param.15) | copy-start | bytes 10756
  66.6 3.1 %collective-permute-start.3 = (f32[3,8,18]{2,1,0:T(8,128)S(1)}, f32[3,8,18]{2,1,0:T(8,128)S(1)}, u32[]{:S(2)}, u32[]{:S(2)}) collective-permute-start(f32[3,8,18]{2,1,0:T(8,128)S(1)} %pad_maximum_fusion.10), channel_id=1, source_target_pairs={{0,1},{1,0},{2,3},{3,2},{4,5},{5,4},{6,7},{7,6},{8,9},{9,8},{10,11... | collective-permute-start | bytes 5192 | tf_op jit(solution)/shard_map/ppermute | solution.py:22
  69.9 6.4 %collective-permute-start.4 = (f32[3,8,153]{2,1,0:T(8,128)S(1)}, f32[3,8,153]{2,1,0:T(8,128)S(1)}, u32[]{:S(2)}, u32[]{:S(2)}) collective-permute-start(f32[3,8,153]{2,1,0:T(8,128)S(1)} %pad_maximum_fusion.1), channel_id=1, source_target_pairs={{0,16},{16,32},{32,48},{48,64},{64,80},{80,96},{96,112},{112,128},... | collective-permute-start | bytes 44072 | tf_op jit(solution)/shard_map/ppermute | solution.py:22
  76.5 6.2 %collective-permute-start.5 = (f32[3,8,34]{2,1,0:T(8,128)S(1)}, f32[3,8,34]{2,1,0:T(8,128)S(1)}, u32[]{:S(2)}, u32[]{:S(2)}) collective-permute-start(f32[3,8,34]{2,1,0:T(8,128)S(1)} %pad_maximum_fusion.11), channel_id=1, source_target_pairs={{0,2},{2,4},{4,6},{6,8},{8,10},{10,12},{12,14},{14,0},{1,3},{3,5},... | collective-permute-start | bytes 9800 | tf_op jit(solution)/shard_map/ppermute | solution.py:22
  78.7 11.7 %copy-start.5 = (f32[3,8,128]{2,1,0:T(8,128)S(1)}, f32[3,8,128]{2,1,0:T(8,128)}, u32[]{:S(2)}) copy-start(f32[3,8,128]{2,1,0:T(8,128)} %param.12) | copy-start | bytes 36868
  92.1 4.5 %collective-permute-start.6 = (f32[3,8,34]{2,1,0:T(8,128)S(1)}, f32[3,8,34]{2,1,0:T(8,128)S(1)}, u32[]{:S(2)}, u32[]{:S(2)}) collective-permute-start(f32[3,8,34]{2,1,0:T(8,128)S(1)} %pad_maximum_fusion.12), channel_id=1, source_target_pairs={{0,14},{2,0},{4,2},{6,4},{8,6},{10,8},{12,10},{14,12},{1,15},{3,1}... | collective-permute-start | bytes 9800 | tf_op jit(solution)/shard_map/ppermute | solution.py:22
  96.8 4.6 %collective-permute-start.7 = (f32[3,8,153]{2,1,0:T(8,128)S(1)}, f32[3,8,153]{2,1,0:T(8,128)S(1)}, u32[]{:S(2)}, u32[]{:S(2)}) collective-permute-start(f32[3,8,153]{2,1,0:T(8,128)S(1)} %pad_maximum_fusion.2), channel_id=1, source_target_pairs={{0,240},{16,0},{32,16},{48,32},{64,48},{80,64},{96,80},{112,96},{1... | collective-permute-start | bytes 44072 | tf_op jit(solution)/shard_map/ppermute | solution.py:22
  101.6 7.1 %collective-permute-start.8 = (f32[3,8,18]{2,1,0:T(8,128)S(1)}, f32[3,8,18]{2,1,0:T(8,128)S(1)}, u32[]{:S(2)}, u32[]{:S(2)}) collective-permute-start(f32[3,8,18]{2,1,0:T(8,128)S(1)} %pad_maximum_fusion.13), channel_id=1, source_target_pairs={{0,1},{1,0},{2,3},{3,2},{4,5},{5,4},{6,7},{7,6},{8,9},{9,8},{10,11... | collective-permute-start | bytes 5192 | tf_op jit(solution)/shard_map/ppermute | solution.py:22
  113.9 3.1 %collective-permute-start.9 = (f32[3,8,18]{2,1,0:T(8,128)S(1)}, f32[3,8,18]{2,1,0:T(8,128)S(1)}, u32[]{:S(2)}, u32[]{:S(2)}) collective-permute-start(f32[3,8,18]{2,1,0:T(8,128)S(1)} %pad_maximum_fusion.14), channel_id=1, source_target_pairs={{0,1},{1,0},{2,3},{3,2},{4,5},{5,4},{6,7},{7,6},{8,9},{9,8},{10,11... | collective-permute-start | bytes 5192 | tf_op jit(solution)/shard_map/ppermute | solution.py:22
  117.2 6.1 %collective-permute-start.10 = (f32[3,8,153]{2,1,0:T(8,128)S(1)}, f32[3,8,153]{2,1,0:T(8,128)S(1)}, u32[]{:S(2)}, u32[]{:S(2)}) collective-permute-start(f32[3,8,153]{2,1,0:T(8,128)S(1)} %pad_maximum_fusion.3), channel_id=1, source_target_pairs={{0,16},{16,32},{32,48},{48,64},{64,80},{80,96},{96,112},{112,128},... | collective-permute-start | bytes 44072 | tf_op jit(solution)/shard_map/ppermute | solution.py:22
  123.5 6.0 %collective-permute-start.11 = (f32[3,8,34]{2,1,0:T(8,128)S(1)}, f32[3,8,34]{2,1,0:T(8,128)S(1)}, u32[]{:S(2)}, u32[]{:S(2)}) collective-permute-start(f32[3,8,34]{2,1,0:T(8,128)S(1)} %pad_maximum_fusion.15), channel_id=1, source_target_pairs={{0,2},{2,4},{4,6},{6,8},{8,10},{10,12},{12,14},{14,0},{1,3},{3,5},... | collective-permute-start | bytes 9800 | tf_op jit(solution)/shard_map/ppermute | solution.py:22
  138.9 4.5 %collective-permute-start.12 = (f32[3,8,34]{2,1,0:T(8,128)S(1)}, f32[3,8,34]{2,1,0:T(8,128)S(1)}, u32[]{:S(2)}, u32[]{:S(2)}) collective-permute-start(f32[3,8,34]{2,1,0:T(8,128)S(1)} %pad_maximum_fusion.16), channel_id=1, source_target_pairs={{0,14},{2,0},{4,2},{6,4},{8,6},{10,8},{12,10},{14,12},{1,15},{3,1}... | collective-permute-start | bytes 9800 | tf_op jit(solution)/shard_map/ppermute | solution.py:22
  143.6 4.6 %collective-permute-start.13 = (f32[3,8,153]{2,1,0:T(8,128)S(1)}, f32[3,8,153]{2,1,0:T(8,128)S(1)}, u32[]{:S(2)}, u32[]{:S(2)}) collective-permute-start(f32[3,8,153]{2,1,0:T(8,128)S(1)} %pad_maximum_fusion.4), channel_id=1, source_target_pairs={{0,240},{16,0},{32,16},{48,32},{64,48},{80,64},{96,80},{112,96},{1... | collective-permute-start | bytes 44072 | tf_op jit(solution)/shard_map/ppermute | solution.py:22
  148.3 7.1 %collective-permute-start.14 = (f32[3,8,18]{2,1,0:T(8,128)S(1)}, f32[3,8,18]{2,1,0:T(8,128)S(1)}, u32[]{:S(2)}, u32[]{:S(2)}) collective-permute-start(f32[3,8,18]{2,1,0:T(8,128)S(1)} %pad_maximum_fusion.17), channel_id=1, source_target_pairs={{0,1},{1,0},{2,3},{3,2},{4,5},{5,4},{6,7},{7,6},{8,9},{9,8},{10,11... | collective-permute-start | bytes 5192 | tf_op jit(solution)/shard_map/ppermute | solution.py:22
  160.7 3.1 %collective-permute-start.15 = (f32[3,8,18]{2,1,0:T(8,128)S(1)}, f32[3,8,18]{2,1,0:T(8,128)S(1)}, u32[]{:S(2)}, u32[]{:S(2)}) collective-permute-start(f32[3,8,18]{2,1,0:T(8,128)S(1)} %pad_maximum_fusion.18), channel_id=1, source_target_pairs={{0,1},{1,0},{2,3},{3,2},{4,5},{5,4},{6,7},{7,6},{8,9},{9,8},{10,11... | collective-permute-start | bytes 5192 | tf_op jit(solution)/shard_map/ppermute | solution.py:22
  164.0 6.1 %collective-permute-start.16 = (f32[3,8,153]{2,1,0:T(8,128)S(1)}, f32[3,8,153]{2,1,0:T(8,128)S(1)}, u32[]{:S(2)}, u32[]{:S(2)}) collective-permute-start(f32[3,8,153]{2,1,0:T(8,128)S(1)} %pad_maximum_fusion.5), channel_id=1, source_target_pairs={{0,16},{16,32},{32,48},{48,64},{64,80},{80,96},{96,112},{112,128},... | collective-permute-start | bytes 44072 | tf_op jit(solution)/shard_map/ppermute | solution.py:22
  170.2 5.9 %collective-permute-start.17 = (f32[3,8,34]{2,1,0:T(8,128)S(1)}, f32[3,8,34]{2,1,0:T(8,128)S(1)}, u32[]{:S(2)}, u32[]{:S(2)}) collective-permute-start(f32[3,8,34]{2,1,0:T(8,128)S(1)} %pad_maximum_fusion.19), channel_id=1, source_target_pairs={{0,2},{2,4},{4,6},{6,8},{8,10},{10,12},{12,14},{14,0},{1,3},{3,5},... | collective-permute-start | bytes 9800 | tf_op jit(solution)/shard_map/ppermute | solution.py:22
  184.8 47.3 %copy-start.2 = (f32[3,8,128]{2,1,0:T(8,128)}, f32[3,8,128]{2,1,0:T(8,128)S(1)}, u32[]{:S(2)}) copy-start(f32[3,8,128]{2,1,0:T(8,128)S(1)} %pad_add_fusion) | copy-start | bytes 36868
  186.2 4.5 %collective-permute-start.18 = (f32[3,8,34]{2,1,0:T(8,128)S(1)}, f32[3,8,34]{2,1,0:T(8,128)S(1)}, u32[]{:S(2)}, u32[]{:S(2)}) collective-permute-start(f32[3,8,34]{2,1,0:T(8,128)S(1)} %pad_maximum_fusion.20), channel_id=1, source_target_pairs={{0,14},{2,0},{4,2},{6,4},{8,6},{10,8},{12,10},{14,12},{1,15},{3,1}... | collective-permute-start | bytes 9800 | tf_op jit(solution)/shard_map/ppermute | solution.py:22
  190.9 4.6 %collective-permute-start.19 = (f32[3,8,153]{2,1,0:T(8,128)S(1)}, f32[3,8,153]{2,1,0:T(8,128)S(1)}, u32[]{:S(2)}, u32[]{:S(2)}) collective-permute-start(f32[3,8,153]{2,1,0:T(8,128)S(1)} %pad_maximum_fusion.6), channel_id=1, source_target_pairs={{0,240},{16,0},{32,16},{48,32},{64,48},{80,64},{96,80},{112,96},{1... | collective-permute-start | bytes 44072 | tf_op jit(solution)/shard_map/ppermute | solution.py:22
  195.7 7.1 %collective-permute-start.20 = (f32[3,8,18]{2,1,0:T(8,128)S(1)}, f32[3,8,18]{2,1,0:T(8,128)S(1)}, u32[]{:S(2)}, u32[]{:S(2)}) collective-permute-start(f32[3,8,18]{2,1,0:T(8,128)S(1)} %pad_maximum_fusion.21), channel_id=1, source_target_pairs={{0,1},{1,0},{2,3},{3,2},{4,5},{5,4},{6,7},{7,6},{8,9},{9,8},{10,11... | collective-permute-start | bytes 5192 | tf_op jit(solution)/shard_map/ppermute | solution.py:22
  208.9 3.1 %collective-permute-start.21 = (f32[3,8,18]{2,1,0:T(8,128)S(1)}, f32[3,8,18]{2,1,0:T(8,128)S(1)}, u32[]{:S(2)}, u32[]{:S(2)}) collective-permute-start(f32[3,8,18]{2,1,0:T(8,128)S(1)} %pad_maximum_fusion.22), channel_id=1, source_target_pairs={{0,1},{1,0},{2,3},{3,2},{4,5},{5,4},{6,7},{7,6},{8,9},{9,8},{10,11... | collective-permute-start | bytes 5192 | tf_op jit(solution)/shard_map/ppermute | solution.py:22
  212.2 6.1 %collective-permute-start.22 = (f32[3,8,153]{2,1,0:T(8,128)S(1)}, f32[3,8,153]{2,1,0:T(8,128)S(1)}, u32[]{:S(2)}, u32[]{:S(2)}) collective-permute-start(f32[3,8,153]{2,1,0:T(8,128)S(1)} %pad_maximum_fusion.7), channel_id=1, source_target_pairs={{0,16},{16,32},{32,48},{48,64},{64,80},{80,96},{96,112},{112,128},... | collective-permute-start | bytes 44072 | tf_op jit(solution)/shard_map/ppermute | solution.py:22
  218.4 6.0 %collective-permute-start.23 = (f32[3,8,34]{2,1,0:T(8,128)S(1)}, f32[3,8,34]{2,1,0:T(8,128)S(1)}, u32[]{:S(2)}, u32[]{:S(2)}) collective-permute-start(f32[3,8,34]{2,1,0:T(8,128)S(1)} %pad_maximum_fusion.23), channel_id=1, source_target_pairs={{0,2},{2,4},{4,6},{6,8},{8,10},{10,12},{12,14},{14,0},{1,3},{3,5},... | collective-permute-start | bytes 9800 | tf_op jit(solution)/shard_map/ppermute | solution.py:22
where the time goes:
time: 285 us; the launch traced here: 284 us
  starting transfers between devices  119 us (42%)
  blocking collectives  49.5 us (17%)
  waiting for transfers between devices  42.6 us (15%)
  other arithmetic  38.8 us (14%)
  matrix products  15.5 us (5%)
  local copies, waits for them, and re-layouts  13.6 us (5%)
  between operations  5.59 us (2%)
    ppermute x24, starting transfers between devices, from_behind(): lax.ppermute(value, axis, [(i, (i + by) % count) for i in range(count)])  119 us
    psum x3, blocking collectives, over_axes(): value = lax.psum(value, axis)  49.5 us
    ppermute x24, waiting for transfers between devices, from_behind(): lax.ppermute(value, axis, [(i, (i + by) % count) for i in range(count)])  42.6 us
    scatter-add x4, other arithmetic, local_forces(): home_forces = forces[:, :, :cluster_count].at[:, :, send_list].add(returned)  28.6 us
  transfers between devices with their start and end apart: 24, of which 24 were waited for; matrix products, arithmetic and copies ran while one was open for 1% of the time, Pallas kernels for 0%

commit v1 on v0

v1 whole, which is shorter than its diff:
```python
import functools

import jax
import jax.numpy as jnp
from jax import lax
from jax.experimental import pallas as pl
from jax.experimental.pallas import tpu as pltpu
from jax.sharding import PartitionSpec as P

CX, CY, CZ = 1, 8, 16
ITERS = 3
NORDER = 4
time_step = 0.02
root_half = 0.7071067811865476
MESH = pl.DeviceIdType.MESH
ZONES = ((1, 0, 0), (0, 1, 0), (0, 0, 1), (1, 1, 0), (1, 0, 1), (0, 1, 1), (1, 1, 1))
AXES = ("gx", "gy", "gz")
FIRST, SECOND = 24, 26
GROUPS = 14
SLOTS = 1792
F32 = jnp.float32


def roll(x, by, axis):
    size = x.shape[axis]
    by = by % size
    return x if by == 0 else pltpu.roll(x, by, axis)


def partners(sizes):
    found = set()
    for zone in ZONES:
        for sign in (1, -1):
            found.add(tuple((sign * z) % n for z, n in zip(zone, sizes)))
    for oy in range(sizes[1]):
        for oz in range(sizes[2]):
            found.add((0, oy, oz))
    for ox in range(sizes[0]):
        found.add((ox, 0, 0))
    found.discard((0, 0, 0))
    return sorted(found)


def lanes(rows=8):
    return lax.broadcasted_iota(jnp.int32, (rows, 128), 1)


def pack(parts):
    lane = lanes()
    one = jnp.where(
        lane < FIRST,
        parts[0],
        jnp.where(lane < 2 * FIRST, roll(parts[1], FIRST, 1), roll(parts[2], 2 * FIRST, 1)),
    )
    two = jnp.where(
        lane < FIRST + SECOND,
        parts[0],
        jnp.where(
            lane < FIRST + 2 * SECOND, roll(parts[1], SECOND, 1), roll(parts[2], 2 * SECOND, 1)
        ),
    )
    return one, two


def unpack(received):
    lane = lanes()
    within = lax.rem(lane, FIRST)
    one = jnp.where(within < 16, received[0], received[1])
    within = lax.rem(lane + (SECOND - FIRST % SECOND), SECOND)
    two = jnp.where(
        within < 16,
        received[2],
        jnp.where(
            within < 24, received[3], jnp.where(within < 25, received[4], received[5])
        ),
    )
    blocks = []
    for c in range(3):
        block = jnp.where(lane < FIRST, roll(one, -FIRST * c, 1), roll(two, -SECOND * c, 1))
        blocks.append(jnp.where(lane < FIRST + SECOND, block, 0.0))
    return blocks


def halves(value):
    high = value.astype(jnp.bfloat16).astype(F32)
    return jnp.concatenate([high, value - high], axis=0).astype(jnp.bfloat16)


def pick(table, index):
    return jnp.take_along_axis(table, index, axis=1, mode="promise_in_bounds")


def up(x):
    return roll(x, -1, 0)


def down(x):
    return roll(x, 1, 0)


def expand(coupling, coupling_down, source):
    series = source
    result = source
    for _ in range(NORDER):
        series = coupling_down * down(series) + coupling * up(series)
        result = result + series
    return result


def dot3(a, b):
    return a[0] * b[0] + a[1] * b[1] + a[2] * b[2]


def constrain(previous, updated, rest, flags, flags_pair):
    old = [x - up(x) for x in previous]
    length = jnp.maximum(jnp.sqrt(dot3(old, old)), 0.2)
    direction = [x / length for x in old]
    coupling = 0.5 * dot3(direction, [up(x) for x in direction]) * flags_pair
    coupling_down = down(coupling)
    links = [x - up(x) for x in updated]
    solution = expand(
        coupling, coupling_down, flags * root_half * (dot3(direction, links) - rest)
    )
    shifts = [x * (root_half * solution) for x in direction]
    updated = [x - s + down(s) for x, s in zip(updated, shifts)]
    links = [x - up(x) for x in updated]
    squared = dot3(links, links)
    target = jnp.sqrt(jnp.maximum(2.0 * rest * rest - squared, 0.25 * rest * rest))
    solution = expand(coupling, coupling_down, flags * root_half * (rest - target))
    shifts = [x * (root_half * solution) for x in direction]
    return [x - s + down(s) for x, s in zip(updated, shifts)]


def kernel(
    sizes,
    pos_ref,
    vel_ref,
    send_ref,
    pair_ref,
    flag_ref,
    out_pos,
    out_vel,
    out_en,
    cur,
    half_ref,
    rest_ref,
    ids,
    send_ids,
    flag8,
    table,
    back,
    near,
    pair_x,
    pair_f,
    coord_x,
    coord_m,
    force_x,
    force_m,
    got_x,
    got_m,
    ret_x,
    ret_m,
    row,
    plane,
    mid,
    line,
    c_send,
    c_recv,
    f_send,
    f_recv,
    p_send,
    p_recv,
    l_send,
    l_recv,
):
    me = tuple(lax.axis_index(a) for a in AXES)

    def at(offset):
        return {
            a: lax.rem(me[i] + (offset[i] % sizes[i]), sizes[i])
            for i, a in enumerate(AXES)
            if offset[i] % sizes[i]
        }

    barrier = pltpu.get_barrier_semaphore()
    others = partners(sizes)
    for offset in others:
        pl.semaphore_signal(barrier, inc=1, device_id=at(offset), device_id_type=MESH)

    lane = lanes()
    ids[...] = jnp.full(ids.shape, CL_PAD, jnp.int32)
    for g in range(GROUPS):
        for side in range(2):
            ids[pl.ds(16 * side + g, 1), :] = pair_ref[pl.ds(side, 1), pl.ds(128 * g, 128)]
    send_ids[...] = jnp.full(send_ids.shape, -1, jnp.int32)
    send_ids[pl.ds(0, 1), :] = send_ref[:, pl.ds(0, 128)]
    send_ids[pl.ds(1, 1), pl.ds(0, FIRST + SECOND)] = send_ref[:, pl.ds(128, FIRST + SECOND)]
    flag8[...] = jnp.zeros(flag8.shape, F32)
    flag8[pl.ds(0, 7), :] = flag_ref[...].astype(F32)
    columns = jnp.transpose(ids[...].astype(F32))
    send_columns = jnp.transpose(send_ids[...].astype(F32))
    wide = lax.broadcasted_iota(jnp.int32, (128, 384), 1).astype(F32)
    for side in range(2):
        value = 12.0 if side == 0 else -12.0
        for g in range(GROUPS):
            column = columns[:, 16 * side + g : 16 * side + g + 1]
            table[pl.ds(128 * (GROUPS * side + g), 128), :] = jnp.where(
                wide == column, value, 0.0
            ).astype(jnp.bfloat16)
    for b in range(2):
        back[pl.ds(128 * b, 128), :] = jnp.where(
            wide[:, :128] == send_columns[:, b : b + 1], 1.0, 0.0
        ).astype(jnp.bfloat16)

    rest_parts = []
    for c in range(3):
        start = pos_ref[c]
        cur[pl.ds(8 * c, 8), :] = start
        half_ref[pl.ds(8 * c, 8), :] = vel_ref[c]
        rest_parts.append(start - up(start))
    rest_ref[...] = jnp.sqrt(dot3(rest_parts, rest_parts))
    row[...] = jnp.zeros(row.shape, F32)

    pl.semaphore_wait(barrier, len(others))

    def coord_copies():
        copies = []
        for number, zone in enumerate(ZONES):
            source = coord_x if number == 0 else coord_m.at[0 if number < 3 else 1]
            target = got_x if number == 0 else got_m.at[number - 1]
            copies.append(
                pltpu.make_async_remote_copy(
                    src_ref=source,
                    dst_ref=target,
                    send_sem=c_send.at[number],
                    recv_sem=c_recv.at[number],
                    device_id=at(tuple(-z for z in zone)),
                    device_id_type=MESH,
                )
            )
        return copies

    def force_copies():
        copies = []
        for number, zone in enumerate(ZONES):
            source = force_x if number == 0 else force_m.at[0 if number < 3 else 1]
            target = ret_x if number == 0 else ret_m.at[number - 1]
            copies.append(
                pltpu.make_async_remote_copy(
                    src_ref=source,
                    dst_ref=target,
                    send_sem=f_send.at[number],
                    recv_sem=f_recv.at[number],
                    device_id=at(zone),
                    device_id_type=MESH,
                )
            )
        return copies

    def step(t, carry):
        send_x = jnp.broadcast_to(send_ids[pl.ds(0, 1), :], (8, 128))
        send_m = jnp.maximum(jnp.broadcast_to(send_ids[pl.ds(1, 1), :], (8, 128)), 0)
        home = [cur[pl.ds(8 * c, 8), :] for c in range(3)]
        chosen = [pick(x, send_m) for x in home]
        in_zone = [(lane >= a) & (lane < b) for a, b in ((0, 16), (16, 24), (24, 40), (40, 48), (48, 49), (49, 50))]
        for c, length in enumerate((CX, CY, CZ)):
            shifted = None
            for number in range(1, 7):
                if ZONES[number][c]:
                    mask = in_zone[number - 1]
                    shifted = mask if shifted is None else shifted | mask
            chosen[c] = chosen[c] + jnp.where(shifted, F32(length), 0.0)
        one, two = pack(chosen)
        coord_m[0] = one
        coord_m[1] = two
        for c in range(3):
            value = pick(home[c], send_x)
            coord_x[pl.ds(8 * c, 8), :] = value + F32(CX) if c == 0 else value
        copies = coord_copies()
        for copy in copies[::-1]:
            copy.start()

        index = [[ids[pl.ds(16 * side + 8 * h, 8), :] for h in range(2)] for side in range(2)]
        low = [[index[s][h] & 127 for h in range(2)] for s in range(2)]
        for r in range(24):
            source = jnp.broadcast_to(cur[pl.ds(r, 1), :], (8, 128))
            for s in range(2):
                for h in range(2):
                    pair_x[s, h, r] = pick(source, low[s][h])

        for copy in copies:
            copy.wait_recv()
        blocks = unpack([got_m[n] for n in range(6)])
        for c in range(3):
            near[pl.ds(8 * c, 8), :] = blocks[c]
        in_home = [[index[s][h] < 128 for h in range(2)] for s in range(2)]
        in_x = [[index[s][h] < 256 for h in range(2)] for s in range(2)]
        for r in range(24):
            source1 = jnp.broadcast_to(got_x[pl.ds(r, 1), :], (8, 128))
            source2 = jnp.broadcast_to(near[pl.ds(r, 1), :], (8, 128))
            for s in range(2):
                for h in range(2):
                    pair_x[s, h, r] = jnp.where(
                        in_home[s][h],
                        pair_x[s, h, r],
                        jnp.where(
                            in_x[s][h], pick(source1, low[s][h]), pick(source2, low[s][h])
                        ),
                    )

        energy = jnp.zeros((8, 128), F32)
        for h in range(2):
            usable = jnp.where(index[0][h] == CL_PAD, 0.0, 1.0)
            distinct = jnp.where(index[0][h] == index[1][h], 0.0, usable)
            second = [[None] * 3 for _ in range(8)]
            for k in range(8):
                xi = [pair_x[0, h, 8 * c + k] for c in range(3)]
                first = [None] * 3
                for l in range(8):
                    d = [xi[c] - pair_x[1, h, 8 * c + l] for c in range(3)]
                    u = jnp.maximum((usable if k < l else distinct) - dot3(d, d), 0.0)
                    uu = u * u
                    energy = energy + uu * u
                    for c in range(3):
                        push = uu * d[c]
                        first[c] = push if l == 0 else first[c] + push
                        second[l][c] = push if k == 0 else second[l][c] + push
                for c in range(3):
                    pair_f[pl.ds((8 * c + k) * 16 + 8 * h, 8), :] = first[c]
            for l in range(8):
                for c in range(3):
                    pair_f[pl.ds(384 + (8 * c + l) * 16 + 8 * h, 8), :] = second[l][c]

        left = jnp.concatenate(
            [
                halves(pair_f[pl.ds(384 * side + g, 24, stride=16), :])
                for side in range(2)
                for g in range(GROUPS)
            ],
            axis=1,
        )

        @pl.when(t > 0)
        def _():
            for copy in force_copies():
                copy.wait_send()

        halo = jnp.dot(left, table[:, pl.ds(128, 256)], preferred_element_type=F32)
        halo = halo[:24] + halo[24:]
        one, two = pack([halo[8 * c : 8 * c + 8, 128:] for c in range(3)])
        force_m[0] = one
        force_m[1] = two
        force_x[...] = halo[:, :128]
        returns = force_copies()
        for copy in returns[::-1]:
            copy.start()

        own = jnp.dot(left, table[:, pl.ds(0, 128)], preferred_element_type=F32)
        own = own[:24] + own[24:]
        total = jnp.sum(jnp.sum(energy, axis=0, keepdims=True), axis=1, keepdims=True)
        row[...] = jnp.where(lanes(1) == 2 * t - 2, 2.0 * total, row[...])
        for copy in copies:
            copy.wait_send()
        for copy in returns:
            copy.wait_recv()
        blocks = unpack([ret_m[n] for n in range(6)])
        came = jnp.concatenate([ret_x[...], jnp.concatenate(blocks, axis=0)], axis=1)
        came = jnp.dot(halves(came), back[...], preferred_element_type=F32)
        force = own + came[:24] + came[24:]
        force = [0.5 * time_step * force[8 * c : 8 * c + 8] for c in range(3)]

        again = jnp.where(t > 0, 1.0, 0.0).astype(F32)
        speed = [half_ref[pl.ds(8 * c, 8), :] + again * force[c] for c in range(3)]
        total = jnp.sum(jnp.sum(dot3(speed, speed), axis=0, keepdims=True), axis=1, keepdims=True)
        row[...] = jnp.where(lanes(1) == 2 * t - 1, 0.5 * total, row[...])

        @pl.when(t < ITERS)
        def _():
            flags = flag8[...]
            half = [speed[c] + force[c] for c in range(3)]
            before = [cur[pl.ds(8 * c, 8), :] for c in range(3)]
            moved = constrain(
                before,
                [x + time_step * v for x, v in zip(before, half)],
                rest_ref[...],
                flags,
                flags * up(flags),
            )
            for c in range(3):
                cur[pl.ds(8 * c, 8), :] = moved[c]
                half_ref[pl.ds(8 * c, 8), :] = (moved[c] - before[c]) / time_step

        @pl.when(t == ITERS)
        def _():
            for c in range(3):
                out_pos[c] = cur[pl.ds(8 * c, 8), :]
                out_vel[c] = speed[c]

        return carry

    lax.fori_loop(0, ITERS + 1, step, 0)
    for copy in force_copies():
        copy.wait_send()

    def gather(source, slots, offsets, own, send, recv):
        copies = []
        for number, offset in enumerate(offsets):
            copies.append(
                pltpu.make_async_remote_copy(
                    src_ref=source,
                    dst_ref=slots.at[own],
                    send_sem=send.at[number],
                    recv_sem=recv.at[number],
                    device_id=at(offset),
                    device_id_type=MESH,
                )
            )
        for copy in copies:
            copy.start()
        slots[own] = source[...]
        for copy in copies:
            copy.wait_recv()
        total = slots[0]
        for n in range(1, slots.shape[0]):
            total = total + slots[n]
        return total, copies

    offsets = [
        (0, y, z) for y in range(sizes[1]) for z in range(sizes[2]) if (y, z) != (0, 0)
    ]
    total, first_copies = gather(row, plane, offsets, me[1] * sizes[2] + me[2], p_send, p_recv)
    mid[...] = total
    offsets = [(x, 0, 0) for x in range(1, sizes[0])]
    total, second_copies = gather(mid, line, offsets, me[0], l_send, l_recv)
    total = total / F32(8 * 128 * sizes[0] * sizes[1] * sizes[2])
    for t in range(ITERS):
        out_en[pl.ds(t, 1), :] = total[:, 2 * t : 2 * t + 2]
    for copy in first_copies + second_copies:
        copy.wait_send()


CL_PAD = 306


def on_device(sizes, positions, velocities, send_list, pair_list, constraint_flags):
    dma = pltpu.SemaphoreType.DMA
    vmem = pltpu.VMEM
    plane = sizes[1] * sizes[2]
    return pl.pallas_call(
        functools.partial(kernel, sizes),
        out_shape=(
            jax.ShapeDtypeStruct((3, 8, 128), F32),
            jax.ShapeDtypeStruct((3, 8, 128), F32),
            jax.ShapeDtypeStruct((ITERS, 2), F32),
        ),
        in_specs=[pl.BlockSpec(memory_space=vmem)] * 5,
        out_specs=[pl.BlockSpec(memory_space=vmem)] * 3,
        scratch_shapes=[
            vmem((24, 128), F32),
            vmem((24, 128), F32),
            vmem((8, 128), F32),
            vmem((32, 128), jnp.int32),
            vmem((8, 128), jnp.int32),
            vmem((8, 128), F32),
            vmem((2 * SLOTS, 384), jnp.bfloat16),
            vmem((256, 128), jnp.bfloat16),
            vmem((24, 128), F32),
            vmem((2, 2, 24, 8, 128), F32),
            vmem((768, 128), F32),
            vmem((24, 128), F32),
            vmem((2, 8, 128), F32),
            vmem((24, 128), F32),
            vmem((2, 8, 128), F32),
            vmem((24, 128), F32),
            vmem((6, 8, 128), F32),
            vmem((24, 128), F32),
            vmem((6, 8, 128), F32),
            vmem((1, 128), F32),
            vmem((plane, 1, 128), F32),
            vmem((1, 128), F32),
            vmem((sizes[0], 1, 128), F32),
            dma((7,)),
            dma((7,)),
            dma((7,)),
            dma((7,)),
            dma((plane - 1,)),
            dma((plane - 1,)),
            dma((sizes[0] - 1,)),
            dma((sizes[0] - 1,)),
        ],
        compiler_params=pltpu.CompilerParams(collective_id=0, has_side_effects=True),
        name="membrane",
    )(positions, velocities, send_list.reshape(1, -1), pair_list, constraint_flags)


def solution(mesh):
    sizes = tuple(mesh.shape[a] for a in AXES)
    spec = ("runs", "gx", "gy", "gz")
    return jax.shard_map(
        functools.partial(on_device, sizes),
        mesh=mesh,
        in_specs=(
            P(None, None, spec),
            P(None, None, spec),
            P(spec),
            P(None, spec),
            P(None, spec),
        ),
        out_specs=(P(None, None, spec), P(None, None, spec), P("runs", None)),
        check_vma=False,
    )
```

time: 285 us -> 109 us (0.38)
  starting transfers between devices: 119 us -> 0 us
  Pallas kernels: 0 us -> 105 us
  blocking collectives: 49.5 us -> 0 us
  waiting for transfers between devices: 42.6 us -> 0 us
  other arithmetic: 38.8 us -> 0 us
  matrix products: 15.5 us -> 0 us
  local copies, waits for them, and re-layouts: 13.6 us -> 3.23 us
  between operations: 5.59 us -> 0.65 us
    ppermute x24 -> x0, starting transfers between devices: 119 us -> none  [from_behind(): lax.ppermute(value, axis, [(i, (i + by) % count) for i in range(count)])]
    pallas_call x0 -> x1, Pallas kernels: none -> 105 us  [on_device(): pl.pallas_call(functools.partial(kernel, sizes), out_shape=(jax.ShapeDtyp...]
    psum x3 -> x0, blocking collectives: 49.5 us -> none  [over_axes(): value = lax.psum(value, axis)]
    ppermute x24 -> x0, waiting for transfers between devices: 42.6 us -> none  [from_behind(): lax.ppermute(value, axis, [(i, (i + by) % count) for i in range(count)])]
    scatter-add x4 -> x0, other arithmetic: 28.6 us -> none  [local_forces(): home_forces = forces[:, :, :cluster_count].at[:, :, send_list].add(returned)]
    dot_general x16 -> x0, matrix products: 15.5 us -> none  [the longest x4 4.36 us: domain_forces(): lax.dot_general(on_first, tables[0], contract, precision=lax.Precision.HI...]
    reduce_sum x23 -> x0, other arithmetic: 5.62 us -> none  [the longest x4 1.95 us: domain_forces(): on_first = jnp.sum(pushing, axis=2).reshape(24, slot_count)]
    slice x93 -> x0, local copies, waits for them, and re-layouts: 5.04 us -> none  [the longest x92 5 us: split_blocks(): pieces.append(packed[:, :, position:position + length])]
  transfers between devices with their start and end apart: 24 -> 0, of which waited for: 24 -> 0; matrix products, arithmetic and copies ran while one was open for 1% -> 0% of each run, Pallas kernels for 0% -> 0%
where the time goes in v1:
time: 109 us
  Pallas kernels  105 us (96%)
  local copies, waits for them, and re-layouts  3.23 us (3%)
    pallas_call x1, Pallas kernels, on_device(): pl.pallas_call(functools.partial(kernel, sizes), out_shape=(jax.ShapeDtyp...  105 us
    unnamed x6, local copies, waits for them, and re-layouts  2.58 us

profile of v1, /device:TPU:65, one launch (start us, length us, event | category | flops | bytes accessed | tf_op | source)
XLA Modules:
  0.0 109.0 jit_solution(591109470959805119)
XLA Ops:
  0.6 105.1 %membrane.1 = (f32[3,8,128]{2,1,0:T(8,128)}, f32[3,8,128]{2,1,0:T(8,128)}, f32[3,2]{1,0:T(4,128)}) custom-call(f32[3,8,128]{2,1,0:T(8,128)} %pos_ref.1, f32[3,8,128]{2,1,0:T(8,128)} %vel_ref.1, s32[1,178]{1,0:T(1,128)} %bitcast.1, s32[2,1792]{1,0:T(2,128)} %pair_ref.1, s32[7,128]{1,0:T(8,128)} %flag_ref.1), custom_call_target="tpu_custom_call" | custom-call | tf_op jit(solution)/shard_map/membrane/pallas_call | solution.py:449
  105.7 0.0 copy-start.1
  105.7 0.7 copy-done.1
  106.4 0.6 copy.8
  107.1 0.0 copy-start
  107.1 1.3 %copy.11 = f32[3,8,128]{2,1,0:T(8,128)} copy(f32[3,8,128]{2,1,0:T(8,128)} %get-tuple-element.9) | data formatting | bytes 24576
  108.4 0.0 copy-done
  108.4 0.6 copy.12
Async XLA Ops:
  105.7 0.7 copy-start.1
  107.1 1.3 %copy-start = (f32[3,8,128]{2,1,0:T(8,128)S(1)}, f32[3,8,128]{2,1,0:T(8,128)}, u32[]{:S(2)}) copy-start(f32[3,8,128]{2,1,0:T(8,128)} %get-tuple-element.10) | copy-start | bytes 36868

commit v2 on v1

--- a/solution.py
+++ b/solution.py
@@ -32,11 +32,6 @@
     for zone in ZONES:
         for sign in (1, -1):
             found.add(tuple((sign * z) % n for z, n in zip(zone, sizes)))
-    for oy in range(sizes[1]):
-        for oz in range(sizes[2]):
-            found.add((0, oy, oz))
-    for ox in range(sizes[0]):
-        found.add((ox, 0, 0))
     found.discard((0, 0, 0))
     return sorted(found)
 
@@ -172,6 +167,7 @@
     p_recv,
     l_send,
     l_recv,
+    token,
 ):
     me = tuple(lax.axis_index(a) for a in AXES)
 
@@ -188,40 +184,51 @@
         pl.semaphore_signal(barrier, inc=1, device_id=at(offset), device_id_type=MESH)
 
     lane = lanes()
-    ids[...] = jnp.full(ids.shape, CL_PAD, jnp.int32)
-    for g in range(GROUPS):
-        for side in range(2):
-            ids[pl.ds(16 * side + g, 1), :] = pair_ref[pl.ds(side, 1), pl.ds(128 * g, 128)]
     send_ids[...] = jnp.full(send_ids.shape, -1, jnp.int32)
     send_ids[pl.ds(0, 1), :] = send_ref[:, pl.ds(0, 128)]
     send_ids[pl.ds(1, 1), pl.ds(0, FIRST + SECOND)] = send_ref[:, pl.ds(128, FIRST + SECOND)]
-    flag8[...] = jnp.zeros(flag8.shape, F32)
-    flag8[pl.ds(0, 7), :] = flag_ref[...].astype(F32)
-    columns = jnp.transpose(ids[...].astype(F32))
-    send_columns = jnp.transpose(send_ids[...].astype(F32))
-    wide = lax.broadcasted_iota(jnp.int32, (128, 384), 1).astype(F32)
-    for side in range(2):
-        value = 12.0 if side == 0 else -12.0
+    for c in range(3):
+        cur[pl.ds(8 * c, 8), :] = pos_ref[c]
+        half_ref[pl.ds(8 * c, 8), :] = vel_ref[c]
+    row[...] = jnp.zeros(row.shape, F32)
+
+    pl.semaphore_wait(barrier, len(others))
+
+    def prepare():
+        ids[...] = jnp.full(ids.shape, CL_PAD, jnp.int32)
         for g in range(GROUPS):
-            column = columns[:, 16 * side + g : 16 * side + g + 1]
-            table[pl.ds(128 * (GROUPS * side + g), 128), :] = jnp.where(
-                wide == column, value, 0.0
+            for side in range(2):
+                ids[pl.ds(16 * side + g, 1), :] = pair_ref[pl.ds(side, 1), pl.ds(128 * g, 128)]
+        flag8[...] = jnp.zeros(flag8.shape, F32)
+        flag8[pl.ds(0, 7), :] = flag_ref[...].astype(F32)
+        columns = jnp.transpose(ids[...].astype(F32))
+        send_columns = jnp.transpose(send_ids[...].astype(F32))
+        wide = lax.broadcasted_iota(jnp.int32, (128, 384), 1).astype(F32)
+        for side in range(2):
+            value = 12.0 if side == 0 else -12.0
+            for g in range(GROUPS):
+                column = columns[:, 16 * side + g : 16 * side + g + 1]
+                table[pl.ds(128 * (GROUPS * side + g), 128), :] = jnp.where(
+                    wide == column, value, 0.0
+                ).astype(jnp.bfloat16)
+        for b in range(2):
+            back[pl.ds(128 * b, 128), :] = jnp.where(
+                wide[:, :128] == send_columns[:, b : b + 1], 1.0, 0.0
             ).astype(jnp.bfloat16)
-    for b in range(2):
-        back[pl.ds(128 * b, 128), :] = jnp.where(
-            wide[:, :128] == send_columns[:, b : b + 1], 1.0, 0.0
-        ).astype(jnp.bfloat16)
-
-    rest_parts = []
-    for c in range(3):
-        start = pos_ref[c]
-        cur[pl.ds(8 * c, 8), :] = start
-        half_ref[pl.ds(8 * c, 8), :] = vel_ref[c]
-        rest_parts.append(start - up(start))
-    rest_ref[...] = jnp.sqrt(dot3(rest_parts, rest_parts))
-    row[...] = jnp.zeros(row.shape, F32)
-
-    pl.semaphore_wait(barrier, len(others))
+        links = [pos_ref[c] - up(pos_ref[c]) for c in range(3)]
+        rest_ref[...] = jnp.sqrt(dot3(links, links))
+
+    ring = [tuple(sign if a == axis else 0 for a in range(3)) for axis in (0, 1) for sign in (1, -1)]
+
+    def tell():
+        for number, offset in enumerate(ring):
+            pl.semaphore_signal(
+                token.at[number], inc=1, device_id=at(offset), device_id_type=MESH
+            )
+
+    def hear():
+        for number in range(len(ring)):
+            pl.semaphore_wait(token.at[number], 1)
 
     def coord_copies():
         copies = []
@@ -273,12 +280,21 @@
         one, two = pack(chosen)
         coord_m[0] = one
         coord_m[1] = two
+        copies = coord_copies()
+        for copy in copies[:0:-1]:
+            copy.start()
         for c in range(3):
             value = pick(home[c], send_x)
             coord_x[pl.ds(8 * c, 8), :] = value + F32(CX) if c == 0 else value
-        copies = coord_copies()
-        for copy in copies[::-1]:
-            copy.start()
+        copies[0].start()
+
+        pl.when(t == 0)(prepare)
+
+        @pl.when(t > 0)
+        def _():
+            hear()
+
+        tell()
 
         index = [[ids[pl.ds(16 * side + 8 * h, 8), :] for h in range(2)] for side in range(2)]
         low = [[index[s][h] & 127 for h in range(2)] for s in range(2)]
@@ -288,24 +304,28 @@
                 for h in range(2):
                     pair_x[s, h, r] = pick(source, low[s][h])
 
-        for copy in copies:
-            copy.wait_recv()
+        in_home = [[index[s][h] < 128 for h in range(2)] for s in range(2)]
+        in_x = [[index[s][h] < 256 for h in range(2)] for s in range(2)]
+        copies[0].wait_recv()
+        for r in range(24):
+            source = jnp.broadcast_to(got_x[pl.ds(r, 1), :], (8, 128))
+            for s in range(2):
+                for h in range(2):
+                    pair_x[s, h, r] = jnp.where(
+                        in_home[s][h], pair_x[s, h, r], pick(source, low[s][h])
+                    )
+
+        for number in (2, 1, 5, 4, 3, 6):
+            copies[number].wait_recv()
         blocks = unpack([got_m[n] for n in range(6)])
         for c in range(3):
             near[pl.ds(8 * c, 8), :] = blocks[c]
-        in_home = [[index[s][h] < 128 for h in range(2)] for s in range(2)]
-        in_x = [[index[s][h] < 256 for h in range(2)] for s in range(2)]
         for r in range(24):
-            source1 = jnp.broadcast_to(got_x[pl.ds(r, 1), :], (8, 128))
-            source2 = jnp.broadcast_to(near[pl.ds(r, 1), :], (8, 128))
+            source = jnp.broadcast_to(near[pl.ds(r, 1), :], (8, 128))
             for s in range(2):
                 for h in range(2):
                     pair_x[s, h, r] = jnp.where(
-                        in_home[s][h],
-                        pair_x[s, h, r],
-                        jnp.where(
-                            in_x[s][h], pick(source1, low[s][h]), pick(source2, low[s][h])
-                        ),
+                        in_x[s][h], pair_x[s, h, r], pick(source, low[s][h])
                     )
 
         energy = jnp.zeros((8, 128), F32)
@@ -345,24 +365,31 @@
             for copy in force_copies():
                 copy.wait_send()
 
-        halo = jnp.dot(left, table[:, pl.ds(128, 256)], preferred_element_type=F32)
+        halo = jnp.dot(left, table[:, pl.ds(256, 128)], preferred_element_type=F32)
         halo = halo[:24] + halo[24:]
-        one, two = pack([halo[8 * c : 8 * c + 8, 128:] for c in range(3)])
+        one, two = pack([halo[8 * c : 8 * c + 8] for c in range(3)])
         force_m[0] = one
         force_m[1] = two
-        force_x[...] = halo[:, :128]
         returns = force_copies()
-        for copy in returns[::-1]:
+        for copy in returns[:0:-1]:
             copy.start()
-
-        own = jnp.dot(left, table[:, pl.ds(0, 128)], preferred_element_type=F32)
+        own = jnp.dot(left, table[:, pl.ds(0, 256)], preferred_element_type=F32)
         own = own[:24] + own[24:]
+        force_x[...] = own[:, 128:]
+        own = own[:, :128]
+        returns[0].start()
+        hear()
+
+        @pl.when(t < ITERS)
+        def _():
+            tell()
+
         total = jnp.sum(jnp.sum(energy, axis=0, keepdims=True), axis=1, keepdims=True)
         row[...] = jnp.where(lanes(1) == 2 * t - 2, 2.0 * total, row[...])
         for copy in copies:
             copy.wait_send()
-        for copy in returns:
-            copy.wait_recv()
+        for number in (2, 1, 0, 5, 4, 3, 6):
+            returns[number].wait_recv()
         blocks = unpack([ret_m[n] for n in range(6)])
         came = jnp.concatenate([ret_x[...], jnp.concatenate(blocks, axis=0)], axis=1)
         came = jnp.dot(halves(came), back[...], preferred_element_type=F32)
@@ -403,6 +430,9 @@
         copy.wait_send()
 
     def gather(source, slots, offsets, own, send, recv):
+        offsets = sorted(
+            offsets, key=lambda o: -sum(min(o[a], sizes[a] - o[a]) for a in range(3))
+        )
         copies = []
         for number, offset in enumerate(offsets):
             copies.append(
@@ -487,6 +517,7 @@
             dma((plane - 1,)),
             dma((sizes[0] - 1,)),
             dma((sizes[0] - 1,)),
+            pltpu.SemaphoreType.REGULAR((4,)),
         ],
         compiler_params=pltpu.CompilerParams(collective_id=0, has_side_effects=True),
         name="membrane",

time: 109 us -> 100 us (0.917)
  Pallas kernels: 105 us -> 95.7 us
    pallas_call x1, Pallas kernels: 105 us -> 95.7 us  [on_device(): pl.pallas_call(functools.partial(kernel, sizes), out_shape=(jax.ShapeDtyp...]
where the time goes in v2:
time: 100 us; the launch traced here: 99.6 us
  Pallas kernels  95.7 us (96%)
  local copies, waits for them, and re-layouts  3.23 us (3%)
    pallas_call x1, Pallas kernels, on_device(): pl.pallas_call(functools.partial(kernel, sizes), out_shape=(jax.ShapeDtyp...  95.7 us
    unnamed x6, local copies, waits for them, and re-layouts  2.58 us

profile of v2, /device:TPU:65, one launch (start us, length us, event | category | flops | bytes accessed | tf_op | source)
XLA Modules:
  0.0 99.6 jit_solution(3521754221642611811)
XLA Ops:
  0.6 95.7 %membrane.1 = (f32[3,8,128]{2,1,0:T(8,128)}, f32[3,8,128]{2,1,0:T(8,128)}, f32[3,2]{1,0:T(4,128)}) custom-call(f32[3,8,128]{2,1,0:T(8,128)} %pos_ref.1, f32[3,8,128]{2,1,0:T(8,128)} %vel_ref.1, s32[1,178]{1,0:T(1,128)} %bitcast.1, s32[2,1792]{1,0:T(2,128)} %pair_ref.1, s32[7,128]{1,0:T(8,128)} %flag_ref.1), custom_call_target="tpu_custom_call" | custom-call | tf_op jit(solution)/shard_map/membrane/pallas_call | solution.py:479
  96.3 0.0 copy-start.1
  96.3 0.7 copy-done.1
  97.0 0.6 copy.8
  97.6 0.0 copy-start
  97.6 1.3 %copy.11 = f32[3,8,128]{2,1,0:T(8,128)} copy(f32[3,8,128]{2,1,0:T(8,128)} %get-tuple-element.9) | data formatting | bytes 24576
  99.0 0.0 copy-done
  99.0 0.6 copy.12
Async XLA Ops:
  96.3 0.7 copy-start.1
  97.6 1.3 %copy-start = (f32[3,8,128]{2,1,0:T(8,128)S(1)}, f32[3,8,128]{2,1,0:T(8,128)}, u32[]{:S(2)}) copy-start(f32[3,8,128]{2,1,0:T(8,128)} %get-tuple-element.10) | copy-start | bytes 36868

commit v3 on v2

--- a/solution.py
+++ b/solution.py
@@ -16,6 +16,7 @@
 ZONES = ((1, 0, 0), (0, 1, 0), (0, 0, 1), (1, 1, 0), (1, 0, 1), (0, 1, 1), (1, 1, 1))
 AXES = ("gx", "gy", "gz")
 FIRST, SECOND = 24, 26
+FAR, NEAR = (3, 6, 4, 5), (1, 2)
 GROUPS = 14
 SLOTS = 1792
 F32 = jnp.float32
@@ -40,21 +41,13 @@
     return lax.broadcasted_iota(jnp.int32, (rows, 128), 1)
 
 
-def pack(parts):
+def side_by_side(parts, first, width):
     lane = lanes()
-    one = jnp.where(
-        lane < FIRST,
+    return jnp.where(
+        lane < first + width,
         parts[0],
-        jnp.where(lane < 2 * FIRST, roll(parts[1], FIRST, 1), roll(parts[2], 2 * FIRST, 1)),
+        jnp.where(lane < first + 2 * width, roll(parts[1], width, 1), roll(parts[2], 2 * width, 1)),
     )
-    two = jnp.where(
-        lane < FIRST + SECOND,
-        parts[0],
-        jnp.where(
-            lane < FIRST + 2 * SECOND, roll(parts[1], SECOND, 1), roll(parts[2], 2 * SECOND, 1)
-        ),
-    )
-    return one, two
 
 
 def unpack(received):
@@ -74,6 +67,10 @@
         block = jnp.where(lane < FIRST, roll(one, -FIRST * c, 1), roll(two, -SECOND * c, 1))
         blocks.append(jnp.where(lane < FIRST + SECOND, block, 0.0))
     return blocks
+
+
+def place(side, g):
+    return 8 * side + g if g < 8 else 16 + (GROUPS - 8) * side + g - 8
 
 
 def halves(value):
@@ -128,11 +125,11 @@
 
 def kernel(
     sizes,
-    pos_ref,
-    vel_ref,
-    send_ref,
-    pair_ref,
-    flag_ref,
+    pos_in,
+    vel_in,
+    send_in,
+    pair_in,
+    flag_in,
     out_pos,
     out_vel,
     out_en,
@@ -168,6 +165,12 @@
     l_send,
     l_recv,
     token,
+    pos_ref,
+    vel_ref,
+    send_ref,
+    pair_ref,
+    flag_ref,
+    loaded,
 ):
     me = tuple(lax.axis_index(a) for a in AXES)
 
@@ -178,23 +181,42 @@
             if offset[i] % sizes[i]
         }
 
+    loads = [
+        pltpu.make_async_copy(source, target, loaded.at[n])
+        for n, (source, target) in enumerate(
+            (
+                (send_in, send_ref),
+                (pos_in, pos_ref),
+                (pair_in, pair_ref),
+                (vel_in, vel_ref),
+                (flag_in, flag_ref),
+            )
+        )
+    ]
+    for load in loads:
+        load.start()
     barrier = pltpu.get_barrier_semaphore()
     others = partners(sizes)
     for offset in others:
         pl.semaphore_signal(barrier, inc=1, device_id=at(offset), device_id_type=MESH)
 
     lane = lanes()
+    row[...] = jnp.zeros(row.shape, F32)
+    loads[0].wait()
+    loads[1].wait()
     send_ids[...] = jnp.full(send_ids.shape, -1, jnp.int32)
     send_ids[pl.ds(0, 1), :] = send_ref[:, pl.ds(0, 128)]
     send_ids[pl.ds(1, 1), pl.ds(0, FIRST + SECOND)] = send_ref[:, pl.ds(128, FIRST + SECOND)]
     for c in range(3):
         cur[pl.ds(8 * c, 8), :] = pos_ref[c]
-        half_ref[pl.ds(8 * c, 8), :] = vel_ref[c]
-    row[...] = jnp.zeros(row.shape, F32)
 
     pl.semaphore_wait(barrier, len(others))
 
     def prepare():
+        for load in loads[2:]:
+            load.wait()
+        for c in range(3):
+            half_ref[pl.ds(8 * c, 8), :] = vel_ref[c]
         ids[...] = jnp.full(ids.shape, CL_PAD, jnp.int32)
         for g in range(GROUPS):
             for side in range(2):
@@ -208,7 +230,7 @@
             value = 12.0 if side == 0 else -12.0
             for g in range(GROUPS):
                 column = columns[:, 16 * side + g : 16 * side + g + 1]
-                table[pl.ds(128 * (GROUPS * side + g), 128), :] = jnp.where(
+                table[pl.ds(128 * place(side, g), 128), :] = jnp.where(
                     wide == column, value, 0.0
                 ).astype(jnp.bfloat16)
         for b in range(2):
@@ -277,12 +299,13 @@
                     mask = in_zone[number - 1]
                     shifted = mask if shifted is None else shifted | mask
             chosen[c] = chosen[c] + jnp.where(shifted, F32(length), 0.0)
-        one, two = pack(chosen)
-        coord_m[0] = one
-        coord_m[1] = two
         copies = coord_copies()
-        for copy in copies[:0:-1]:
-            copy.start()
+        coord_m[1] = side_by_side(chosen, FIRST, SECOND)
+        for number in FAR:
+            copies[number].start()
+        coord_m[0] = side_by_side(chosen, 0, FIRST)
+        for number in NEAR:
+            copies[number].start()
         for c in range(3):
             value = pick(home[c], send_x)
             coord_x[pl.ds(8 * c, 8), :] = value + F32(CX) if c == 0 else value
@@ -293,6 +316,8 @@
         @pl.when(t > 0)
         def _():
             hear()
+            for copy in force_copies():
+                copy.wait_send()
 
         tell()
 
@@ -315,7 +340,7 @@
                         in_home[s][h], pair_x[s, h, r], pick(source, low[s][h])
                     )
 
-        for number in (2, 1, 5, 4, 3, 6):
+        for number in NEAR + FAR:
             copies[number].wait_recv()
         blocks = unpack([got_m[n] for n in range(6)])
         for c in range(3):
@@ -329,6 +354,8 @@
                     )
 
         energy = jnp.zeros((8, 128), F32)
+        lefts = []
+        halo = None
         for h in range(2):
             usable = jnp.where(index[0][h] == CL_PAD, 0.0, 1.0)
             distinct = jnp.where(index[0][h] == index[1][h], 0.0, usable)
@@ -351,33 +378,43 @@
                 for c in range(3):
                     pair_f[pl.ds(384 + (8 * c + l) * 16 + 8 * h, 8), :] = second[l][c]
 
-        left = jnp.concatenate(
-            [
-                halves(pair_f[pl.ds(384 * side + g, 24, stride=16), :])
-                for side in range(2)
-                for g in range(GROUPS)
-            ],
-            axis=1,
-        )
-
-        @pl.when(t > 0)
-        def _():
-            for copy in force_copies():
-                copy.wait_send()
-
-        halo = jnp.dot(left, table[:, pl.ds(256, 128)], preferred_element_type=F32)
+            groups = range(8) if h == 0 else range(8, GROUPS)
+            left = jnp.concatenate(
+                [
+                    halves(pair_f[pl.ds(384 * side + g, 24, stride=16), :])
+                    for side in range(2)
+                    for g in groups
+                ],
+                axis=1,
+            )
+            lefts.append(left)
+            part = jnp.dot(
+                left,
+                table[pl.ds(2048 * h, left.shape[1]), pl.ds(128, 256)],
+                preferred_element_type=F32,
+            )
+            halo = part if h == 0 else halo + part
+
         halo = halo[:24] + halo[24:]
-        one, two = pack([halo[8 * c : 8 * c + 8] for c in range(3)])
-        force_m[0] = one
-        force_m[1] = two
         returns = force_copies()
-        for copy in returns[:0:-1]:
-            copy.start()
-        own = jnp.dot(left, table[:, pl.ds(0, 256)], preferred_element_type=F32)
+        beyond = [halo[8 * c : 8 * c + 8, 128:] for c in range(3)]
+        force_m[1] = side_by_side(beyond, FIRST, SECOND)
+        for number in FAR:
+            returns[number].start()
+        force_m[0] = side_by_side(beyond, 0, FIRST)
+        for number in NEAR:
+            returns[number].start()
+        force_x[...] = halo[:, :128]
+        returns[0].start()
+        own = None
+        for h in range(2):
+            part = jnp.dot(
+                lefts[h],
+                table[pl.ds(2048 * h, lefts[h].shape[1]), pl.ds(0, 128)],
+                preferred_element_type=F32,
+            )
+            own = part if h == 0 else own + part
         own = own[:24] + own[24:]
-        force_x[...] = own[:, 128:]
-        own = own[:, :128]
-        returns[0].start()
         hear()
 
         @pl.when(t < ITERS)
@@ -385,10 +422,10 @@
             tell()
 
         total = jnp.sum(jnp.sum(energy, axis=0, keepdims=True), axis=1, keepdims=True)
-        row[...] = jnp.where(lanes(1) == 2 * t - 2, 2.0 * total, row[...])
+        row[...] = jnp.where(lanes(1) == t - 1, 2.0 * total, row[...])
         for copy in copies:
             copy.wait_send()
-        for number in (2, 1, 0, 5, 4, 3, 6):
+        for number in (0,) + NEAR + FAR:
             returns[number].wait_recv()
         blocks = unpack([ret_m[n] for n in range(6)])
         came = jnp.concatenate([ret_x[...], jnp.concatenate(blocks, axis=0)], axis=1)
@@ -399,7 +436,7 @@
         again = jnp.where(t > 0, 1.0, 0.0).astype(F32)
         speed = [half_ref[pl.ds(8 * c, 8), :] + again * force[c] for c in range(3)]
         total = jnp.sum(jnp.sum(dot3(speed, speed), axis=0, keepdims=True), axis=1, keepdims=True)
-        row[...] = jnp.where(lanes(1) == 2 * t - 1, 0.5 * total, row[...])
+        row[...] = jnp.where(lanes(1) == KINETIC + t - 1, 0.5 * total, row[...])
 
         @pl.when(t < ITERS)
         def _():
@@ -462,28 +499,45 @@
     mid[...] = total
     offsets = [(x, 0, 0) for x in range(1, sizes[0])]
     total, second_copies = gather(mid, line, offsets, me[0], l_send, l_recv)
-    total = total / F32(8 * 128 * sizes[0] * sizes[1] * sizes[2])
-    for t in range(ITERS):
-        out_en[pl.ds(t, 1), :] = total[:, 2 * t : 2 * t + 2]
+    out_en[...] = total
     for copy in first_copies + second_copies:
         copy.wait_send()
 
 
 CL_PAD = 306
+KINETIC = 8
+VMEM_LIMIT = 12 << 20
+
+
+def finish(beads, pos_ref, vel_ref, sum_ref, out_pos, out_vel, out_en, energy, stored):
+    stores = [
+        pltpu.make_async_copy(source, target, stored.at[n])
+        for n, (source, target) in enumerate(
+            ((pos_ref, out_pos), (vel_ref, out_vel), (energy, out_en))
+        )
+    ]
+    stores[0].start()
+    stores[1].start()
+    total = sum_ref[...] / F32(beads)
+    for n in range(2):
+        energy[pl.ds(n, 1), :] = total[:, KINETIC * n : KINETIC * n + ITERS]
+    stores[2].start()
+    for store in stores:
+        store.wait()
 
 
 def on_device(sizes, positions, velocities, send_list, pair_list, constraint_flags):
     dma = pltpu.SemaphoreType.DMA
     vmem = pltpu.VMEM
     plane = sizes[1] * sizes[2]
-    return pl.pallas_call(
+    results = pl.pallas_call(
         functools.partial(kernel, sizes),
         out_shape=(
             jax.ShapeDtypeStruct((3, 8, 128), F32),
             jax.ShapeDtypeStruct((3, 8, 128), F32),
-            jax.ShapeDtypeStruct((ITERS, 2), F32),
+            jax.ShapeDtypeStruct((1, 128), F32),
         ),
-        in_specs=[pl.BlockSpec(memory_space=vmem)] * 5,
+        in_specs=[pl.BlockSpec(memory_space=pltpu.HBM)] * 5,
         out_specs=[pl.BlockSpec(memory_space=vmem)] * 3,
         scratch_shapes=[
             vmem((24, 128), F32),
@@ -518,10 +572,43 @@
             dma((sizes[0] - 1,)),
             dma((sizes[0] - 1,)),
             pltpu.SemaphoreType.REGULAR((4,)),
+            vmem((3, 8, 128), F32),
+            vmem((3, 8, 128), F32),
+            vmem((1, 178), jnp.int32),
+            vmem((2, SLOTS), jnp.int32),
+            vmem((7, 128), jnp.int32),
+            dma((5,)),
         ],
-        compiler_params=pltpu.CompilerParams(collective_id=0, has_side_effects=True),
+        compiler_params=pltpu.CompilerParams(
+            collective_id=0, has_side_effects=True, vmem_limit_bytes=VMEM_LIMIT
+        ),
         name="membrane",
-    )(positions, velocities, send_list.reshape(1, -1), pair_list, constraint_flags)
+    )(
+        *[
+            pltpu.with_memory_space_constraint(x, pltpu.HBM)
+            for x in (
+                positions,
+                velocities,
+                send_list.reshape(1, -1),
+                pair_list,
+                constraint_flags,
+            )
+        ]
+    )
+    position, velocity, energies = pl.pallas_call(
+        functools.partial(finish, 8 * 128 * sizes[0] * sizes[1] * sizes[2]),
+        out_shape=(
+            jax.ShapeDtypeStruct((3, 8, 128), F32),
+            jax.ShapeDtypeStruct((3, 8, 128), F32),
+            jax.ShapeDtypeStruct((2, ITERS), F32),
+        ),
+        in_specs=[pl.BlockSpec(memory_space=vmem)] * 3,
+        out_specs=[pl.BlockSpec(memory_space=pltpu.HBM)] * 3,
+        scratch_shapes=[vmem((2, ITERS), F32), dma((3,))],
+        compiler_params=pltpu.CompilerParams(vmem_limit_bytes=1 << 20),
+        name="finish",
+    )(*results)
+    return position, velocity, energies.T
 
 
 def solution(mesh):

time: 100 us -> 95.6 us (0.956)
  local copies, waits for them, and re-layouts: 3.23 us -> 0 us
  Pallas kernels: 95.7 us -> 94.6 us
    unnamed x6 -> x0, local copies, waits for them, and re-layouts: 2.58 us -> none
    pallas_call x1, Pallas kernels: 95.7 us -> 93.9 us  [on_device(): pl.pallas_call(functools.partial(kernel, sizes), out_shape=(jax.ShapeDtyp...]
where the time goes in v3:
time: 95.6 us; the launch traced here: 95.3 us
  Pallas kernels  94.6 us (99%)
    pallas_call x1, Pallas kernels, on_device(): pl.pallas_call(functools.partial(kernel, sizes), out_shape=(jax.ShapeDtyp...  93.9 us

profile of v3, /device:TPU:65, one launch (start us, length us, event | category | flops | bytes accessed | tf_op | source)
XLA Modules:
  0.0 95.3 jit_solution(6799435641585098626)
XLA Ops:
  0.6 93.9 %membrane.1 = (f32[3,8,128]{2,1,0:T(8,128)S(1)}, f32[3,8,128]{2,1,0:T(8,128)S(1)}, f32[1,128]{1,0:T(1,128)S(1)}) custom-call(f32[3,8,128]{2,1,0:T(8,128)} %pos_in.1, f32[3,8,128]{2,1,0:T(8,128)} %vel_in.1, s32[1,178]{1,0:T(1,128)} %bitcast.2, s32[2,1792]{1,0:T(2,128)} %pair_in.1, s32[7,128]{1,0:T(8,128)} %flag_in.1), custom_call_target="tpu_custom_call" | custom-call | tf_op jit(solution)/shard_map/membrane/pallas_call | solution.py:533
  94.6 0.7 finish.1

commit v4 on v3

--- a/solution.py
+++ b/solution.py
@@ -171,6 +171,9 @@
     pair_ref,
     flag_ref,
     loaded,
+    blocks_ref,
+    rows_ref,
+    speed_ref,
 ):
     me = tuple(lax.axis_index(a) for a in AXES)
 
@@ -261,8 +264,8 @@
                 pltpu.make_async_remote_copy(
                     src_ref=source,
                     dst_ref=target,
-                    send_sem=c_send.at[number],
-                    recv_sem=c_recv.at[number],
+                    send_sem=c_send.at[0 if number == 0 else 1],
+                    recv_sem=c_recv.at[0 if number == 0 else 1],
                     device_id=at(tuple(-z for z in zone)),
                     device_id_type=MESH,
                 )
@@ -278,13 +281,22 @@
                 pltpu.make_async_remote_copy(
                     src_ref=source,
                     dst_ref=target,
-                    send_sem=f_send.at[number],
-                    recv_sem=f_recv.at[number],
+                    send_sem=f_send.at[0 if number == 0 else 1],
+                    recv_sem=f_recv.at[0 if number == 0 else 1],
                     device_id=at(zone),
                     device_id_type=MESH,
                 )
             )
         return copies
+
+    def drain(sem, ref):
+        pltpu.make_async_copy(ref, ref, sem).wait()
+
+    def kinetic(speed, number):
+        total = jnp.sum(
+            jnp.sum(dot3(speed, speed), axis=0, keepdims=True), axis=1, keepdims=True
+        )
+        row[...] = jnp.where(lanes(1) == KINETIC + number, 0.5 * total, row[...])
 
     def step(t, carry):
         send_x = jnp.broadcast_to(send_ids[pl.ds(0, 1), :], (8, 128))
@@ -316,8 +328,9 @@
         @pl.when(t > 0)
         def _():
             hear()
-            for copy in force_copies():
-                copy.wait_send()
+            force_copies()[0].wait_send()
+            drain(f_send.at[1], blocks_ref)
+            kinetic([speed_ref[pl.ds(8 * c, 8), :] for c in range(3)], t - 2)
 
         tell()
 
@@ -340,18 +353,20 @@
                         in_home[s][h], pair_x[s, h, r], pick(source, low[s][h])
                     )
 
-        for number in NEAR + FAR:
-            copies[number].wait_recv()
+        drain(c_recv.at[1], blocks_ref)
         blocks = unpack([got_m[n] for n in range(6)])
         for c in range(3):
             near[pl.ds(8 * c, 8), :] = blocks[c]
-        for r in range(24):
+
+        def complete(r, h):
             source = jnp.broadcast_to(near[pl.ds(r, 1), :], (8, 128))
             for s in range(2):
-                for h in range(2):
-                    pair_x[s, h, r] = jnp.where(
-                        in_x[s][h], pair_x[s, h, r], pick(source, low[s][h])
-                    )
+                pair_x[s, h, r] = jnp.where(
+                    in_x[s][h], pair_x[s, h, r], pick(source, low[s][h])
+                )
+
+        for r in range(24):
+            complete(r, 0)
 
         energy = jnp.zeros((8, 128), F32)
         lefts = []
@@ -374,6 +389,9 @@
                         second[l][c] = push if k == 0 else second[l][c] + push
                 for c in range(3):
                     pair_f[pl.ds((8 * c + k) * 16 + 8 * h, 8), :] = first[c]
+                if h == 0:
+                    for r in range(3 * k, 3 * k + 3):
+                        complete(r, 1)
             for l in range(8):
                 for c in range(3):
                     pair_f[pl.ds(384 + (8 * c + l) * 16 + 8 * h, 8), :] = second[l][c]
@@ -423,20 +441,21 @@
 
         total = jnp.sum(jnp.sum(energy, axis=0, keepdims=True), axis=1, keepdims=True)
         row[...] = jnp.where(lanes(1) == t - 1, 2.0 * total, row[...])
-        for copy in copies:
-            copy.wait_send()
-        for number in (0,) + NEAR + FAR:
-            returns[number].wait_recv()
-        blocks = unpack([ret_m[n] for n in range(6)])
-        came = jnp.concatenate([ret_x[...], jnp.concatenate(blocks, axis=0)], axis=1)
-        came = jnp.dot(halves(came), back[...], preferred_element_type=F32)
+        copies[0].wait_send()
+        drain(c_send.at[1], blocks_ref)
+        returns[0].wait_recv()
+        came = jnp.dot(
+            halves(ret_x[...]), back[pl.ds(0, 128), :], preferred_element_type=F32
+        )
+        own = own + came[:24] + came[24:]
+        drain(f_recv.at[1], blocks_ref)
+        came = jnp.concatenate(unpack([ret_m[n] for n in range(6)]), axis=0)
+        came = jnp.dot(halves(came), back[pl.ds(128, 128), :], preferred_element_type=F32)
         force = own + came[:24] + came[24:]
         force = [0.5 * time_step * force[8 * c : 8 * c + 8] for c in range(3)]
 
         again = jnp.where(t > 0, 1.0, 0.0).astype(F32)
         speed = [half_ref[pl.ds(8 * c, 8), :] + again * force[c] for c in range(3)]
-        total = jnp.sum(jnp.sum(dot3(speed, speed), axis=0, keepdims=True), axis=1, keepdims=True)
-        row[...] = jnp.where(lanes(1) == KINETIC + t - 1, 0.5 * total, row[...])
 
         @pl.when(t < ITERS)
         def _():
@@ -453,9 +472,11 @@
             for c in range(3):
                 cur[pl.ds(8 * c, 8), :] = moved[c]
                 half_ref[pl.ds(8 * c, 8), :] = (moved[c] - before[c]) / time_step
+                speed_ref[pl.ds(8 * c, 8), :] = speed[c]
 
         @pl.when(t == ITERS)
         def _():
+            kinetic(speed, ITERS - 1)
             for c in range(3):
                 out_pos[c] = cur[pl.ds(8 * c, 8), :]
                 out_vel[c] = speed[c]
@@ -463,45 +484,52 @@
         return carry
 
     lax.fori_loop(0, ITERS + 1, step, 0)
-    for copy in force_copies():
-        copy.wait_send()
-
-    def gather(source, slots, offsets, own, send, recv):
-        offsets = sorted(
-            offsets, key=lambda o: -sum(min(o[a], sizes[a] - o[a]) for a in range(3))
-        )
-        copies = []
-        for number, offset in enumerate(offsets):
-            copies.append(
-                pltpu.make_async_remote_copy(
-                    src_ref=source,
-                    dst_ref=slots.at[own],
-                    send_sem=send.at[number],
-                    recv_sem=recv.at[number],
-                    device_id=at(offset),
-                    device_id_type=MESH,
-                )
-            )
-        for copy in copies:
-            copy.start()
-        slots[own] = source[...]
-        for copy in copies:
-            copy.wait_recv()
+    def distance(offset):
+        return sum(min(o, n - o) for o, n in zip(offset, sizes))
+
+    def copy_row(source, target, offset, send, recv):
+        pltpu.make_async_remote_copy(
+            src_ref=source,
+            dst_ref=target,
+            send_sem=send,
+            recv_sem=recv,
+            device_id=at(offset),
+            device_id_type=MESH,
+        ).start()
+
+    def total_of(slots):
         total = slots[0]
         for n in range(1, slots.shape[0]):
             total = total + slots[n]
-        return total, copies
-
-    offsets = [
-        (0, y, z) for y in range(sizes[1]) for z in range(sizes[2]) if (y, z) != (0, 0)
-    ]
-    total, first_copies = gather(row, plane, offsets, me[1] * sizes[2] + me[2], p_send, p_recv)
-    mid[...] = total
-    offsets = [(x, 0, 0) for x in range(1, sizes[0])]
-    total, second_copies = gather(mid, line, offsets, me[0], l_send, l_recv)
-    out_en[...] = total
-    for copy in first_copies + second_copies:
-        copy.wait_send()
+        return total
+
+    offsets = [(0, y, z) for y in range(sizes[1]) for z in range(sizes[2]) if y or z]
+    own = me[1] * sizes[2] + me[2]
+    for offset in sorted(offsets, key=distance, reverse=True):
+        copy_row(row, plane.at[own], offset, p_send.at[0], p_recv.at[0])
+    plane[own] = row[...]
+    force_copies()[0].wait_send()
+    drain(f_send.at[1], blocks_ref)
+    drain(p_recv.at[0], rows_ref.at[pl.ds(0, len(offsets))])
+    mid[...] = total_of(plane)
+    offsets = sorted([(x, 0, 0) for x in range(1, sizes[0])], key=distance)
+    lead = me[2] == sizes[2] - 1
+
+    @pl.when(lead)
+    def _():
+        for x, _, _ in offsets:
+            for z in range(sizes[2]):
+                copy_row(mid, line.at[me[0]], (x, 0, z), l_send.at[z], l_recv.at[0])
+
+    line[me[0]] = mid[...]
+    drain(p_send.at[0], rows_ref.at[pl.ds(0, plane.shape[0] - 1)])
+    drain(l_recv.at[0], rows_ref.at[pl.ds(0, len(offsets))])
+    out_en[...] = total_of(line)
+
+    @pl.when(lead)
+    def _():
+        for z in range(sizes[2]):
+            drain(l_send.at[z], rows_ref.at[pl.ds(0, len(offsets))])
 
 
 CL_PAD = 306
@@ -563,14 +591,14 @@
             vmem((plane, 1, 128), F32),
             vmem((1, 128), F32),
             vmem((sizes[0], 1, 128), F32),
-            dma((7,)),
-            dma((7,)),
-            dma((7,)),
-            dma((7,)),
-            dma((plane - 1,)),
-            dma((plane - 1,)),
-            dma((sizes[0] - 1,)),
-            dma((sizes[0] - 1,)),
+            dma((2,)),
+            dma((2,)),
+            dma((2,)),
+            dma((2,)),
+            dma((1,)),
+            dma((1,)),
+            dma((sizes[2],)),
+            dma((1,)),
             pltpu.SemaphoreType.REGULAR((4,)),
             vmem((3, 8, 128), F32),
             vmem((3, 8, 128), F32),
@@ -578,6 +606,9 @@
             vmem((2, SLOTS), jnp.int32),
             vmem((7, 128), jnp.int32),
             dma((5,)),
+            vmem((6, 8, 128), F32),
+            vmem((max(plane, sizes[0]) - 1, 1, 128), F32),
+            vmem((24, 128), F32),
         ],
         compiler_params=pltpu.CompilerParams(
             collective_id=0, has_side_effects=True, vmem_limit_bytes=VMEM_LIMIT

time: 95.6 us -> 94.1 us (0.984)
  Pallas kernels: 94.6 us -> 93.3 us
    pallas_call x1, Pallas kernels: 93.9 us -> 92.7 us  [on_device(): pl.pallas_call(functools.partial(kernel, sizes), out_shape=(jax.ShapeDtyp...]
where the time goes in v4:
time: 94.1 us; the launch traced here: 94 us
  Pallas kernels  93.3 us (99%)
    pallas_call x1, Pallas kernels, on_device(): pl.pallas_call(functools.partial(kernel, sizes), out_shape=(jax.ShapeDtyp...  92.7 us

profile of v4, /device:TPU:65, one launch (start us, length us, event | category | flops | bytes accessed | tf_op | source)
XLA Modules:
  0.0 94.0 jit_solution(12658819096354853053)
XLA Ops:
  0.6 92.7 %membrane.1 = (f32[3,8,128]{2,1,0:T(8,128)S(1)}, f32[3,8,128]{2,1,0:T(8,128)S(1)}, f32[1,128]{1,0:T(1,128)S(1)}) custom-call(f32[3,8,128]{2,1,0:T(8,128)} %pos_in.1, f32[3,8,128]{2,1,0:T(8,128)} %vel_in.1, s32[1,178]{1,0:T(1,128)} %bitcast.2, s32[2,1792]{1,0:T(2,128)} %pair_in.1, s32[7,128]{1,0:T(8,128)} %flag_in.1), custom_call_target="tpu_custom_call" | custom-call | tf_op jit(solution)/shard_map/membrane/pallas_call | solution.py:561
  93.3 0.7 finish.1

commit v5 on v4

--- a/solution.py
+++ b/solution.py
@@ -34,7 +34,7 @@
         for sign in (1, -1):
             found.add(tuple((sign * z) % n for z, n in zip(zone, sizes)))
     found.discard((0, 0, 0))
-    return sorted(found)
+    return sorted(found, key=lambda o: (-sum(min(a, n - a) for a, n in zip(o, sizes)), o))
 
 
 def lanes(rows=8):
@@ -50,23 +50,18 @@
     )
 
 
-def unpack(received):
-    lane = lanes()
-    within = lax.rem(lane, FIRST)
-    one = jnp.where(within < 16, received[0], received[1])
-    within = lax.rem(lane + (SECOND - FIRST % SECOND), SECOND)
-    two = jnp.where(
+def merge_near(received):
+    within = lax.rem(lanes(), FIRST)
+    return jnp.where(within < 16, received[0], received[1])
+
+
+def merge_far(received):
+    within = lax.rem(lanes() + (SECOND - FIRST % SECOND), SECOND)
+    return jnp.where(
         within < 16,
-        received[2],
-        jnp.where(
-            within < 24, received[3], jnp.where(within < 25, received[4], received[5])
-        ),
+        received[0],
+        jnp.where(within < 24, received[1], jnp.where(within < 25, received[2], received[3])),
     )
-    blocks = []
-    for c in range(3):
-        block = jnp.where(lane < FIRST, roll(one, -FIRST * c, 1), roll(two, -SECOND * c, 1))
-        blocks.append(jnp.where(lane < FIRST + SECOND, block, 0.0))
-    return blocks
 
 
 def place(side, g):
@@ -90,35 +85,58 @@
     return roll(x, 1, 0)
 
 
-def expand(coupling, coupling_down, source):
-    series = source
-    result = source
-    for _ in range(NORDER):
-        series = coupling_down * down(series) + coupling * up(series)
-        result = result + series
-    return result
-
-
 def dot3(a, b):
     return a[0] * b[0] + a[1] * b[1] + a[2] * b[2]
 
 
-def constrain(previous, updated, rest, flags, flags_pair):
+def lag(x, by):
+    return roll(x, -by, 0)
+
+
+def expansion(coupling):
+    coupling_down = down(coupling)
+    power = {0: None}
+    weights = {0: jnp.ones(coupling.shape, F32)}
+    for _ in range(NORDER):
+        later = {}
+        for m, weight in power.items():
+            lower = coupling_down if weight is None else coupling_down * down(weight)
+            upper = coupling if weight is None else coupling * up(weight)
+            for where_to, term in ((m - 1, lower), (m + 1, upper)):
+                later[where_to] = later[where_to] + term if where_to in later else term
+        power = later
+        for m, weight in power.items():
+            weights[m] = weights[m] + weight if m in weights else weight
+    return [weights[m] for m in range(-NORDER, NORDER + 1)]
+
+
+def expand(weights, source):
+    terms = [w * lag(source, m - NORDER) for m, w in enumerate(weights)]
+    while len(terms) > 1:
+        terms = [
+            terms[n] + terms[n + 1] if n + 1 < len(terms) else terms[n]
+            for n in range(0, len(terms), 2)
+        ]
+    return terms[0]
+
+
+def link_frame(previous, flags_pair):
     old = [x - up(x) for x in previous]
     length = jnp.maximum(jnp.sqrt(dot3(old, old)), 0.2)
     direction = [x / length for x in old]
     coupling = 0.5 * dot3(direction, [up(x) for x in direction]) * flags_pair
-    coupling_down = down(coupling)
+    return direction, expansion(coupling)
+
+
+def constrain(updated, direction, weights, rest, flags):
     links = [x - up(x) for x in updated]
-    solution = expand(
-        coupling, coupling_down, flags * root_half * (dot3(direction, links) - rest)
-    )
+    solution = expand(weights, flags * root_half * (dot3(direction, links) - rest))
     shifts = [x * (root_half * solution) for x in direction]
     updated = [x - s + down(s) for x, s in zip(updated, shifts)]
     links = [x - up(x) for x in updated]
     squared = dot3(links, links)
     target = jnp.sqrt(jnp.maximum(2.0 * rest * rest - squared, 0.25 * rest * rest))
-    solution = expand(coupling, coupling_down, flags * root_half * (rest - target))
+    solution = expand(weights, flags * root_half * (rest - target))
     shifts = [x * (root_half * solution) for x in direction]
     return [x - s + down(s) for x, s in zip(updated, shifts)]
 
@@ -141,7 +159,9 @@
     flag8,
     table,
     back,
+    back2,
     near,
+    frame,
     pair_x,
     pair_f,
     coord_x,
@@ -196,12 +216,14 @@
             )
         )
     ]
-    for load in loads:
+    for load in loads[:2]:
         load.start()
     barrier = pltpu.get_barrier_semaphore()
     others = partners(sizes)
     for offset in others:
         pl.semaphore_signal(barrier, inc=1, device_id=at(offset), device_id_type=MESH)
+    for load in loads[2:]:
+        load.start()
 
     lane = lanes()
     row[...] = jnp.zeros(row.shape, F32)
@@ -212,8 +234,6 @@
     send_ids[pl.ds(1, 1), pl.ds(0, FIRST + SECOND)] = send_ref[:, pl.ds(128, FIRST + SECOND)]
     for c in range(3):
         cur[pl.ds(8 * c, 8), :] = pos_ref[c]
-
-    pl.semaphore_wait(barrier, len(others))
 
     def prepare():
         for load in loads[2:]:
@@ -227,6 +247,12 @@
         flag8[...] = jnp.zeros(flag8.shape, F32)
         flag8[pl.ds(0, 7), :] = flag_ref[...].astype(F32)
         columns = jnp.transpose(ids[...].astype(F32))
+        entry = jnp.broadcast_to(send_ids[pl.ds(1, 1), :], (8, 128))
+        goals = [entry + 128 * c for c in range(3)]
+        for n, (first, width) in enumerate(((0, FIRST), (FIRST, SECOND))):
+            goal = side_by_side(goals, first, width)
+            goal = jnp.where((lane >= first) & (lane < first + 3 * width), goal, -1)
+            send_ids[pl.ds(2 + n, 1), :] = goal[:1]
         send_columns = jnp.transpose(send_ids[...].astype(F32))
         wide = lax.broadcasted_iota(jnp.int32, (128, 384), 1).astype(F32)
         for side in range(2):
@@ -236,9 +262,10 @@
                 table[pl.ds(128 * place(side, g), 128), :] = jnp.where(
                     wide == column, value, 0.0
                 ).astype(jnp.bfloat16)
+        back[...] = jnp.where(wide[:, :128] == send_columns[:, 0:1], 1.0, 0.0).astype(jnp.bfloat16)
         for b in range(2):
-            back[pl.ds(128 * b, 128), :] = jnp.where(
-                wide[:, :128] == send_columns[:, b : b + 1], 1.0, 0.0
+            back2[pl.ds(128 * b, 128), :] = jnp.where(
+                wide == send_columns[:, 2 + b : 3 + b], 1.0, 0.0
             ).astype(jnp.bfloat16)
         links = [pos_ref[c] - up(pos_ref[c]) for c in range(3)]
         rest_ref[...] = jnp.sqrt(dot3(links, links))
@@ -265,7 +292,7 @@
                     src_ref=source,
                     dst_ref=target,
                     send_sem=c_send.at[0 if number == 0 else 1],
-                    recv_sem=c_recv.at[0 if number == 0 else 1],
+                    recv_sem=c_recv.at[0 if number == 0 else 1 if number in NEAR else 2],
                     device_id=at(tuple(-z for z in zone)),
                     device_id_type=MESH,
                 )
@@ -298,21 +325,22 @@
         )
         row[...] = jnp.where(lanes(1) == KINETIC + number, 0.5 * total, row[...])
 
-    def step(t, carry):
+    def send_coords(home, ready=None):
         send_x = jnp.broadcast_to(send_ids[pl.ds(0, 1), :], (8, 128))
         send_m = jnp.maximum(jnp.broadcast_to(send_ids[pl.ds(1, 1), :], (8, 128)), 0)
-        home = [cur[pl.ds(8 * c, 8), :] for c in range(3)]
         chosen = [pick(x, send_m) for x in home]
-        in_zone = [(lane >= a) & (lane < b) for a, b in ((0, 16), (16, 24), (24, 40), (40, 48), (48, 49), (49, 50))]
+        edges = (0, 16, 24, 40, 48, 49, 50)
         for c, length in enumerate((CX, CY, CZ)):
             shifted = None
             for number in range(1, 7):
                 if ZONES[number][c]:
-                    mask = in_zone[number - 1]
+                    mask = (lane >= edges[number - 1]) & (lane < edges[number])
                     shifted = mask if shifted is None else shifted | mask
             chosen[c] = chosen[c] + jnp.where(shifted, F32(length), 0.0)
         copies = coord_copies()
         coord_m[1] = side_by_side(chosen, FIRST, SECOND)
+        if ready is not None:
+            ready()
         for number in FAR:
             copies[number].start()
         coord_m[0] = side_by_side(chosen, 0, FIRST)
@@ -323,6 +351,12 @@
             coord_x[pl.ds(8 * c, 8), :] = value + F32(CX) if c == 0 else value
         copies[0].start()
 
+    send_coords(
+        [pos_ref[c] for c in range(3)], lambda: pl.semaphore_wait(barrier, len(others))
+    )
+
+    def step(t, carry):
+        copies = coord_copies()
         pl.when(t == 0)(prepare)
 
         @pl.when(t > 0)
@@ -353,20 +387,40 @@
                         in_home[s][h], pair_x[s, h, r], pick(source, low[s][h])
                     )
 
-        drain(c_recv.at[1], blocks_ref)
-        blocks = unpack([got_m[n] for n in range(6)])
-        for c in range(3):
-            near[pl.ds(8 * c, 8), :] = blocks[c]
-
-        def complete(r, h):
-            source = jnp.broadcast_to(near[pl.ds(r, 1), :], (8, 128))
-            for s in range(2):
-                pair_x[s, h, r] = jnp.where(
-                    in_x[s][h], pair_x[s, h, r], pick(source, low[s][h])
-                )
-
-        for r in range(24):
-            complete(r, 0)
+        drain(c_recv.at[1], blocks_ref.at[pl.ds(0, 2)])
+        in_near = [[index[s][h] < 256 + FIRST for h in range(2)] for s in range(2)]
+
+        def places(width):
+            return [[[(low[s][h] + width * c) & 127 for c in range(3)] for h in range(2)] for s in range(2)]
+
+        near_place, far_place = places(FIRST), places(SECOND)
+        near[pl.ds(0, 8), :] = merge_near([got_m[n] for n in range(2)])
+        for k in range(8):
+            source = jnp.broadcast_to(near[pl.ds(k, 1), :], (8, 128))
+            for c in range(3):
+                for s in range(2):
+                    for h in range(2):
+                        pair_x[s, h, 8 * c + k] = jnp.where(
+                            in_x[s][h],
+                            pair_x[s, h, 8 * c + k],
+                            pick(source, near_place[s][h][c]),
+                        )
+
+        drain(c_recv.at[2], blocks_ref.at[pl.ds(0, 4)])
+        near[pl.ds(8, 8), :] = merge_far([got_m[n] for n in range(2, 6)])
+
+        def complete(k, h):
+            source = jnp.broadcast_to(near[pl.ds(8 + k, 1), :], (8, 128))
+            for c in range(3):
+                for s in range(2):
+                    pair_x[s, h, 8 * c + k] = jnp.where(
+                        in_near[s][h],
+                        pair_x[s, h, 8 * c + k],
+                        pick(source, far_place[s][h][c]),
+                    )
+
+        for k in range(8):
+            complete(k, 0)
 
         energy = jnp.zeros((8, 128), F32)
         lefts = []
@@ -390,8 +444,7 @@
                 for c in range(3):
                     pair_f[pl.ds((8 * c + k) * 16 + 8 * h, 8), :] = first[c]
                 if h == 0:
-                    for r in range(3 * k, 3 * k + 3):
-                        complete(r, 1)
+                    complete(k, 1)
             for l in range(8):
                 for c in range(3):
                     pair_f[pl.ds(384 + (8 * c + l) * 16 + 8 * h, 8), :] = second[l][c]
@@ -441,34 +494,45 @@
 
         total = jnp.sum(jnp.sum(energy, axis=0, keepdims=True), axis=1, keepdims=True)
         row[...] = jnp.where(lanes(1) == t - 1, 2.0 * total, row[...])
+        flags = flag8[...]
+        direction, weights = link_frame(
+            [cur[pl.ds(8 * c, 8), :] for c in range(3)], flags * up(flags)
+        )
+        for n, value in enumerate(direction + weights):
+            frame[pl.ds(8 * n, 8), :] = value
+
         copies[0].wait_send()
         drain(c_send.at[1], blocks_ref)
         returns[0].wait_recv()
         came = jnp.dot(
-            halves(ret_x[...]), back[pl.ds(0, 128), :], preferred_element_type=F32
+            halves(ret_x[...]), back[...], preferred_element_type=F32
         )
         own = own + came[:24] + came[24:]
         drain(f_recv.at[1], blocks_ref)
-        came = jnp.concatenate(unpack([ret_m[n] for n in range(6)]), axis=0)
-        came = jnp.dot(halves(came), back[pl.ds(128, 128), :], preferred_element_type=F32)
-        force = own + came[:24] + came[24:]
-        force = [0.5 * time_step * force[8 * c : 8 * c + 8] for c in range(3)]
+        received = [ret_m[n] for n in range(6)]
+        came = jnp.concatenate([merge_near(received[:2]), merge_far(received[2:])], axis=1)
+        came = jnp.dot(halves(came), back2[...], preferred_element_type=F32)
+        came = came[:8] + came[8:]
+        force = [
+            0.5 * time_step * (own[8 * c : 8 * c + 8] + came[:, 128 * c : 128 * c + 128])
+            for c in range(3)
+        ]
 
         again = jnp.where(t > 0, 1.0, 0.0).astype(F32)
         speed = [half_ref[pl.ds(8 * c, 8), :] + again * force[c] for c in range(3)]
 
         @pl.when(t < ITERS)
         def _():
-            flags = flag8[...]
             half = [speed[c] + force[c] for c in range(3)]
             before = [cur[pl.ds(8 * c, 8), :] for c in range(3)]
             moved = constrain(
-                before,
                 [x + time_step * v for x, v in zip(before, half)],
+                [frame[pl.ds(8 * n, 8), :] for n in range(3)],
+                [frame[pl.ds(8 * n, 8), :] for n in range(3, 3 + 2 * NORDER + 1)],
                 rest_ref[...],
-                flags,
-                flags * up(flags),
-            )
+                flag8[...],
+            )
+            send_coords(moved)
             for c in range(3):
                 cur[pl.ds(8 * c, 8), :] = moved[c]
                 half_ref[pl.ds(8 * c, 8), :] = (moved[c] - before[c]) / time_step
@@ -575,8 +639,10 @@
             vmem((8, 128), jnp.int32),
             vmem((8, 128), F32),
             vmem((2 * SLOTS, 384), jnp.bfloat16),
-            vmem((256, 128), jnp.bfloat16),
-            vmem((24, 128), F32),
+            vmem((128, 128), jnp.bfloat16),
+            vmem((256, 384), jnp.bfloat16),
+            vmem((16, 128), F32),
+            vmem((24 + 8 * (2 * NORDER + 1), 128), F32),
             vmem((2, 2, 24, 8, 128), F32),
             vmem((768, 128), F32),
             vmem((24, 128), F32),
@@ -592,7 +658,7 @@
             vmem((1, 128), F32),
             vmem((sizes[0], 1, 128), F32),
             dma((2,)),
-            dma((2,)),
+            dma((3,)),
             dma((2,)),
             dma((2,)),
             dma((1,)),

time: 94.1 us -> 93.7 us (level)
  no operation moved by 1% of the time
where the time goes in v5:
time: 93.7 us; the launch traced here: 93.5 us
  Pallas kernels  92.9 us (99%)
    pallas_call x1, Pallas kernels, on_device(): pl.pallas_call(functools.partial(kernel, sizes), out_shape=(jax.ShapeDtyp...  92.2 us

profile of v5, /device:TPU:65, one launch (start us, length us, event | category | flops | bytes accessed | tf_op | source)
XLA Modules:
  0.0 93.5 jit_solution(7311263585182889295)
XLA Ops:
  0.6 92.2 %membrane.1 = (f32[3,8,128]{2,1,0:T(8,128)S(1)}, f32[3,8,128]{2,1,0:T(8,128)S(1)}, f32[1,128]{1,0:T(1,128)S(1)}) custom-call(f32[3,8,128]{2,1,0:T(8,128)} %pos_in.1, f32[3,8,128]{2,1,0:T(8,128)} %vel_in.1, s32[1,178]{1,0:T(1,128)} %bitcast.2, s32[2,1792]{1,0:T(2,128)} %pair_in.1, s32[7,128]{1,0:T(8,128)} %flag_in.1), custom_call_target="tpu_custom_call" | custom-call | tf_op jit(solution)/shard_map/membrane/pallas_call | solution.py:625
  92.8 0.7 finish.1

commit v6 on v5

--- a/solution.py
+++ b/solution.py
@@ -19,6 +19,7 @@
 FAR, NEAR = (3, 6, 4, 5), (1, 2)
 GROUPS = 14
 SLOTS = 1792
+PITCH = 24
 F32 = jnp.float32
 
 
@@ -50,18 +51,11 @@
     )
 
 
-def merge_near(received):
-    within = lax.rem(lanes(), FIRST)
-    return jnp.where(within < 16, received[0], received[1])
-
-
-def merge_far(received):
-    within = lax.rem(lanes() + (SECOND - FIRST % SECOND), SECOND)
-    return jnp.where(
-        within < 16,
-        received[0],
-        jnp.where(within < 24, received[1], jnp.where(within < 25, received[2], received[3])),
-    )
+def merge(zone, received):
+    block = received[0]
+    for n in range(1, len(received)):
+        block = jnp.where(zone >= n, received[n], block)
+    return block
 
 
 def place(side, g):
@@ -133,7 +127,7 @@
     solution = expand(weights, flags * root_half * (dot3(direction, links) - rest))
     shifts = [x * (root_half * solution) for x in direction]
     updated = [x - s + down(s) for x, s in zip(updated, shifts)]
-    links = [x - up(x) for x in updated]
+    links = [x - (s + s) + (down(s) + up(s)) for x, s in zip(links, shifts)]
     squared = dot3(links, links)
     target = jnp.sqrt(jnp.maximum(2.0 * rest * rest - squared, 0.25 * rest * rest))
     solution = expand(weights, flags * root_half * (rest - target))
@@ -194,6 +188,8 @@
     blocks_ref,
     rows_ref,
     speed_ref,
+    packed,
+    shift,
 ):
     me = tuple(lax.axis_index(a) for a in AXES)
 
@@ -309,7 +305,7 @@
                     src_ref=source,
                     dst_ref=target,
                     send_sem=f_send.at[0 if number == 0 else 1],
-                    recv_sem=f_recv.at[0 if number == 0 else 1],
+                    recv_sem=f_recv.at[0 if number == 0 else 1 if number in NEAR else 2],
                     device_id=at(zone),
                     device_id_type=MESH,
                 )
@@ -325,25 +321,41 @@
         )
         row[...] = jnp.where(lanes(1) == KINETIC + number, 0.5 * total, row[...])
 
+    edges = (0, 16, 24, 40, 48, 49, 50)
+    entry = jnp.broadcast_to(send_ids[pl.ds(1, 1), :], (8, 128))
+    for n, (first, width) in enumerate(((0, FIRST), (FIRST, SECOND))):
+        zone = jnp.zeros((8, 128), jnp.int32)
+        offset = [jnp.zeros((8, 128), F32) for _ in range(3)]
+        for number in range(1, 7):
+            begin = edges[number - 1]
+            inside = (lane >= begin) & (lane < edges[number])
+            zone = jnp.where(inside, number - 1 if n == 0 else number - 3, zone)
+            for c, length in enumerate((CX, CY, CZ)):
+                if ZONES[number][c]:
+                    offset[c] = jnp.where(inside, F32(length), offset[c])
+        packed[n] = side_by_side([zone] * 3, first, width)
+        packed[2 + n] = jnp.maximum(side_by_side([entry] * 3, first, width), 0)
+        shift[n] = side_by_side(offset, first, width)
+
+    def chosen(n, home):
+        first, width = ((0, FIRST), (FIRST, SECOND))[n]
+        index = packed[2 + n]
+        picked = [pick(x, index) for x in home]
+        return shift[n] + jnp.where(
+            lane < first + width,
+            picked[0],
+            jnp.where(lane < first + 2 * width, picked[1], picked[2]),
+        )
+
     def send_coords(home, ready=None):
         send_x = jnp.broadcast_to(send_ids[pl.ds(0, 1), :], (8, 128))
-        send_m = jnp.maximum(jnp.broadcast_to(send_ids[pl.ds(1, 1), :], (8, 128)), 0)
-        chosen = [pick(x, send_m) for x in home]
-        edges = (0, 16, 24, 40, 48, 49, 50)
-        for c, length in enumerate((CX, CY, CZ)):
-            shifted = None
-            for number in range(1, 7):
-                if ZONES[number][c]:
-                    mask = (lane >= edges[number - 1]) & (lane < edges[number])
-                    shifted = mask if shifted is None else shifted | mask
-            chosen[c] = chosen[c] + jnp.where(shifted, F32(length), 0.0)
         copies = coord_copies()
-        coord_m[1] = side_by_side(chosen, FIRST, SECOND)
+        coord_m[1] = chosen(1, home)
         if ready is not None:
             ready()
         for number in FAR:
             copies[number].start()
-        coord_m[0] = side_by_side(chosen, 0, FIRST)
+        coord_m[0] = chosen(0, home)
         for number in NEAR:
             copies[number].start()
         for c in range(3):
@@ -394,7 +406,7 @@
             return [[[(low[s][h] + width * c) & 127 for c in range(3)] for h in range(2)] for s in range(2)]
 
         near_place, far_place = places(FIRST), places(SECOND)
-        near[pl.ds(0, 8), :] = merge_near([got_m[n] for n in range(2)])
+        near[pl.ds(0, 8), :] = merge(packed[0], [got_m[n] for n in range(2)])
         for k in range(8):
             source = jnp.broadcast_to(near[pl.ds(k, 1), :], (8, 128))
             for c in range(3):
@@ -407,7 +419,7 @@
                         )
 
         drain(c_recv.at[2], blocks_ref.at[pl.ds(0, 4)])
-        near[pl.ds(8, 8), :] = merge_far([got_m[n] for n in range(2, 6)])
+        near[pl.ds(8, 8), :] = merge(packed[1], [got_m[n] for n in range(2, 6)])
 
         def complete(k, h):
             source = jnp.broadcast_to(near[pl.ds(8 + k, 1), :], (8, 128))
@@ -442,17 +454,17 @@
                         first[c] = push if l == 0 else first[c] + push
                         second[l][c] = push if k == 0 else second[l][c] + push
                 for c in range(3):
-                    pair_f[pl.ds((8 * c + k) * 16 + 8 * h, 8), :] = first[c]
+                    pair_f[pl.ds((8 * c + k) * PITCH + 8 * h, 8), :] = first[c]
                 if h == 0:
                     complete(k, 1)
             for l in range(8):
                 for c in range(3):
-                    pair_f[pl.ds(384 + (8 * c + l) * 16 + 8 * h, 8), :] = second[l][c]
+                    pair_f[pl.ds((24 + 8 * c + l) * PITCH + 8 * h, 8), :] = second[l][c]
 
             groups = range(8) if h == 0 else range(8, GROUPS)
             left = jnp.concatenate(
                 [
-                    halves(pair_f[pl.ds(384 * side + g, 24, stride=16), :])
+                    halves(pair_f[pl.ds(24 * PITCH * side + g, 24, stride=PITCH), :])
                     for side in range(2)
                     for g in groups
                 ],
@@ -508,13 +520,19 @@
             halves(ret_x[...]), back[...], preferred_element_type=F32
         )
         own = own + came[:24] + came[24:]
-        drain(f_recv.at[1], blocks_ref)
-        received = [ret_m[n] for n in range(6)]
-        came = jnp.concatenate([merge_near(received[:2]), merge_far(received[2:])], axis=1)
-        came = jnp.dot(halves(came), back2[...], preferred_element_type=F32)
+        drain(f_recv.at[1], blocks_ref.at[pl.ds(0, 2)])
+        came = merge(packed[0], [ret_m[n] for n in range(2)])
+        came = jnp.dot(halves(came), back2[pl.ds(0, 128), :], preferred_element_type=F32)
+        came = came[:8] + came[8:]
+        own = [
+            own[8 * c : 8 * c + 8] + came[:, 128 * c : 128 * c + 128] for c in range(3)
+        ]
+        drain(f_recv.at[2], blocks_ref.at[pl.ds(0, 4)])
+        came = merge(packed[1], [ret_m[n] for n in range(2, 6)])
+        came = jnp.dot(halves(came), back2[pl.ds(128, 128), :], preferred_element_type=F32)
         came = came[:8] + came[8:]
         force = [
-            0.5 * time_step * (own[8 * c : 8 * c + 8] + came[:, 128 * c : 128 * c + 128])
+            0.5 * time_step * (own[c] + came[:, 128 * c : 128 * c + 128])
             for c in range(3)
         ]
 
@@ -644,7 +662,7 @@
             vmem((16, 128), F32),
             vmem((24 + 8 * (2 * NORDER + 1), 128), F32),
             vmem((2, 2, 24, 8, 128), F32),
-            vmem((768, 128), F32),
+            vmem((48 * PITCH, 128), F32),
             vmem((24, 128), F32),
             vmem((2, 8, 128), F32),
             vmem((24, 128), F32),
@@ -660,7 +678,7 @@
             dma((2,)),
             dma((3,)),
             dma((2,)),
-            dma((2,)),
+            dma((3,)),
             dma((1,)),
             dma((1,)),
             dma((sizes[2],)),
@@ -675,6 +693,8 @@
             vmem((6, 8, 128), F32),
             vmem((max(plane, sizes[0]) - 1, 1, 128), F32),
             vmem((24, 128), F32),
+            vmem((4, 8, 128), jnp.int32),
+            vmem((2, 8, 128), F32),
         ],
         compiler_params=pltpu.CompilerParams(
             collective_id=0, has_side_effects=True, vmem_limit_bytes=VMEM_LIMIT

time: 93.7 us -> 93.8 us (level)
  no operation moved by 1% of the time
where the time goes in v6:
time: 93.8 us; the launch traced here: 93.6 us
  Pallas kernels  93 us (99%)
    pallas_call x1, Pallas kernels, on_device(): pl.pallas_call(functools.partial(kernel, sizes), out_shape=(jax.ShapeDtyp...  92.3 us

profile of v6, /device:TPU:65, one launch (start us, length us, event | category | flops | bytes accessed | tf_op | source)
XLA Modules:
  0.0 93.6 jit_solution(12244038268088018696)
XLA Ops:
  0.6 92.3 %membrane.1 = (f32[3,8,128]{2,1,0:T(8,128)S(1)}, f32[3,8,128]{2,1,0:T(8,128)S(1)}, f32[1,128]{1,0:T(1,128)S(1)}) custom-call(f32[3,8,128]{2,1,0:T(8,128)} %pos_in.1, f32[3,8,128]{2,1,0:T(8,128)} %vel_in.1, s32[1,178]{1,0:T(1,128)} %bitcast.2, s32[2,1792]{1,0:T(2,128)} %pair_in.1, s32[7,128]{1,0:T(8,128)} %flag_in.1), custom_call_target="tpu_custom_call" | custom-call | tf_op jit(solution)/shard_map/membrane/pallas_call | solution.py:643
  92.9 0.7 finish.1

commit v7 on v6

--- a/solution.py
+++ b/solution.py
@@ -27,15 +27,6 @@
     size = x.shape[axis]
     by = by % size
     return x if by == 0 else pltpu.roll(x, by, axis)
-
-
-def partners(sizes):
-    found = set()
-    for zone in ZONES:
-        for sign in (1, -1):
-            found.add(tuple((sign * z) % n for z, n in zip(zone, sizes)))
-    found.discard((0, 0, 0))
-    return sorted(found, key=lambda o: (-sum(min(a, n - a) for a, n in zip(o, sizes)), o))
 
 
 def lanes(rows=8):
@@ -215,9 +206,10 @@
     for load in loads[:2]:
         load.start()
     barrier = pltpu.get_barrier_semaphore()
-    others = partners(sizes)
-    for offset in others:
-        pl.semaphore_signal(barrier, inc=1, device_id=at(offset), device_id_type=MESH)
+    for number in FAR + (0,) + NEAR:
+        pl.semaphore_signal(
+            barrier, inc=1, device_id=at(ZONES[number]), device_id_type=MESH
+        )
     for load in loads[2:]:
         load.start()
 
@@ -347,25 +339,31 @@
             jnp.where(lane < first + 2 * width, picked[1], picked[2]),
         )
 
-    def send_coords(home, ready=None):
+    def build_x(home):
         send_x = jnp.broadcast_to(send_ids[pl.ds(0, 1), :], (8, 128))
+        for c in range(3):
+            value = pick(home[c], send_x)
+            coord_x[pl.ds(8 * c, 8), :] = value + F32(CX) if c == 0 else value
+
+    def send_coords(home):
         copies = coord_copies()
         coord_m[1] = chosen(1, home)
-        if ready is not None:
-            ready()
         for number in FAR:
             copies[number].start()
         coord_m[0] = chosen(0, home)
         for number in NEAR:
             copies[number].start()
-        for c in range(3):
-            value = pick(home[c], send_x)
-            coord_x[pl.ds(8 * c, 8), :] = value + F32(CX) if c == 0 else value
+        build_x(home)
         copies[0].start()
 
-    send_coords(
-        [pos_ref[c] for c in range(3)], lambda: pl.semaphore_wait(barrier, len(others))
-    )
+    start = [pos_ref[c] for c in range(3)]
+    coord_m[1] = chosen(1, start)
+    coord_m[0] = chosen(0, start)
+    build_x(start)
+    pl.semaphore_wait(barrier, len(ZONES))
+    copies = coord_copies()
+    for number in FAR + NEAR + (0,):
+        copies[number].start()
 
     def step(t, carry):
         copies = coord_copies()
@@ -373,12 +371,11 @@
 
         @pl.when(t > 0)
         def _():
-            hear()
+            pl.when(t > 1)(hear)
+            tell()
             force_copies()[0].wait_send()
             drain(f_send.at[1], blocks_ref)
             kinetic([speed_ref[pl.ds(8 * c, 8), :] for c in range(3)], t - 2)
-
-        tell()
 
         index = [[ids[pl.ds(16 * side + 8 * h, 8), :] for h in range(2)] for side in range(2)]
         low = [[index[s][h] & 127 for h in range(2)] for s in range(2)]
@@ -436,7 +433,7 @@
 
         energy = jnp.zeros((8, 128), F32)
         lefts = []
-        halo = None
+        parts = []
         for h in range(2):
             usable = jnp.where(index[0][h] == CL_PAD, 0.0, 1.0)
             distinct = jnp.where(index[0][h] == index[1][h], 0.0, usable)
@@ -471,37 +468,39 @@
                 axis=1,
             )
             lefts.append(left)
-            part = jnp.dot(
-                left,
-                table[pl.ds(2048 * h, left.shape[1]), pl.ds(128, 256)],
-                preferred_element_type=F32,
+            parts.append(
+                jnp.dot(
+                    left,
+                    table[pl.ds(2048 * h, left.shape[1]), pl.ds(128 if h == 0 else 256, 256 if h == 0 else 128)],
+                    preferred_element_type=F32,
+                )
             )
-            halo = part if h == 0 else halo + part
-
+
+        halo = parts[0][:, 128:] + parts[1]
         halo = halo[:24] + halo[24:]
         returns = force_copies()
-        beyond = [halo[8 * c : 8 * c + 8, 128:] for c in range(3)]
+        beyond = [halo[8 * c : 8 * c + 8] for c in range(3)]
         force_m[1] = side_by_side(beyond, FIRST, SECOND)
         for number in FAR:
             returns[number].start()
         force_m[0] = side_by_side(beyond, 0, FIRST)
         for number in NEAR:
             returns[number].start()
-        force_x[...] = halo[:, :128]
+        rest = jnp.dot(
+            lefts[1],
+            table[pl.ds(2048, lefts[1].shape[1]), pl.ds(0, 256)],
+            preferred_element_type=F32,
+        )
+        halo = parts[0][:, :128] + rest[:, 128:]
+        force_x[...] = halo[:24] + halo[24:]
         returns[0].start()
-        own = None
-        for h in range(2):
-            part = jnp.dot(
-                lefts[h],
-                table[pl.ds(2048 * h, lefts[h].shape[1]), pl.ds(0, 128)],
-                preferred_element_type=F32,
-            )
-            own = part if h == 0 else own + part
+        own = rest[:, :128] + jnp.dot(
+            lefts[0], table[pl.ds(0, 2048), pl.ds(0, 128)], preferred_element_type=F32
+        )
         own = own[:24] + own[24:]
-        hear()
-
-        @pl.when(t < ITERS)
+        @pl.when(t > 0)
         def _():
+            hear()
             tell()
 
         total = jnp.sum(jnp.sum(energy, axis=0, keepdims=True), axis=1, keepdims=True)
@@ -590,8 +589,11 @@
     for offset in sorted(offsets, key=distance, reverse=True):
         copy_row(row, plane.at[own], offset, p_send.at[0], p_recv.at[0])
     plane[own] = row[...]
+    hear()
+    tell()
     force_copies()[0].wait_send()
     drain(f_send.at[1], blocks_ref)
+    hear()
     drain(p_recv.at[0], rows_ref.at[pl.ds(0, len(offsets))])
     mid[...] = total_of(plane)
     offsets = sorted([(x, 0, 0) for x in range(1, sizes[0])], key=distance)

time: 93.8 us -> 92.8 us (0.989)
  Pallas kernels: 93 us -> 92 us
    pallas_call x1, Pallas kernels: 92.3 us -> 91.3 us  [on_device(): pl.pallas_call(functools.partial(kernel, sizes), out_shape=(jax.ShapeDtyp...]
where the time goes in v7:
time: 92.8 us; the launch traced here: 92.6 us
  Pallas kernels  92 us (99%)
    pallas_call x1, Pallas kernels, on_device(): pl.pallas_call(functools.partial(kernel, sizes), out_shape=(jax.ShapeDtyp...  91.3 us

profile of v7, /device:TPU:65, one launch (start us, length us, event | category | flops | bytes accessed | tf_op | source)
XLA Modules:
  0.0 92.6 jit_solution(2445970049717049795)
XLA Ops:
  0.6 91.3 %membrane.1 = (f32[3,8,128]{2,1,0:T(8,128)S(1)}, f32[3,8,128]{2,1,0:T(8,128)S(1)}, f32[1,128]{1,0:T(1,128)S(1)}) custom-call(f32[3,8,128]{2,1,0:T(8,128)} %pos_in.1, f32[3,8,128]{2,1,0:T(8,128)} %vel_in.1, s32[1,178]{1,0:T(1,128)} %bitcast.2, s32[2,1792]{1,0:T(2,128)} %pair_in.1, s32[7,128]{1,0:T(8,128)} %flag_in.1), custom_call_target="tpu_custom_call" | custom-call | tf_op jit(solution)/shard_map/membrane/pallas_call | solution.py:645
  92.0 0.7 finish.1

commit v8 on v7

--- a/solution.py
+++ b/solution.py
@@ -49,8 +49,30 @@
     return block
 
 
+PASSES = ((0, 8), (8, 4), (12, 2))
+
+
 def place(side, g):
-    return 8 * side + g if g < 8 else 16 + (GROUPS - 8) * side + g - 8
+    for begin, width in PASSES:
+        if g < begin + width:
+            return 2 * begin + width * side + g - begin
+
+
+def pass_of(g):
+    return max(n for n, (begin, _) in enumerate(PASSES) if begin <= g)
+
+
+def where_is(side, p, c, k):
+    width = PASSES[p][1]
+    return sum(3 * w for _, w in PASSES[:p]) + c * width + k if side == 0 else 42 + 24 * p + 8 * c + k
+
+
+def rows_of(row, width, k):
+    sublane = lax.broadcasted_iota(jnp.int32, (8, 128), 0)
+    value = jnp.broadcast_to(row(k), (8, 128))
+    for n in range(1, 8 // width):
+        value = jnp.where(sublane >= n * width, jnp.broadcast_to(row(k + n * width), (8, 128)), value)
+    return value
 
 
 def halves(value):
@@ -228,10 +250,13 @@
             load.wait()
         for c in range(3):
             half_ref[pl.ds(8 * c, 8), :] = vel_ref[c]
-        ids[...] = jnp.full(ids.shape, CL_PAD, jnp.int32)
-        for g in range(GROUPS):
-            for side in range(2):
-                ids[pl.ds(16 * side + g, 1), :] = pair_ref[pl.ds(side, 1), pl.ds(128 * g, 128)]
+        for side in range(2):
+            for p, (begin, width) in enumerate(PASSES):
+                for n in range(8):
+                    g = begin + n % width
+                    ids[pl.ds(24 * side + 8 * p + n, 1), :] = pair_ref[
+                        pl.ds(side, 1), pl.ds(128 * g, 128)
+                    ]
         flag8[...] = jnp.zeros(flag8.shape, F32)
         flag8[pl.ds(0, 7), :] = flag_ref[...].astype(F32)
         columns = jnp.transpose(ids[...].astype(F32))
@@ -246,7 +271,8 @@
         for side in range(2):
             value = 12.0 if side == 0 else -12.0
             for g in range(GROUPS):
-                column = columns[:, 16 * side + g : 16 * side + g + 1]
+                at_row = 24 * side + 8 * pass_of(g) + g - PASSES[pass_of(g)][0]
+                column = columns[:, at_row : at_row + 1]
                 table[pl.ds(128 * place(side, g), 128), :] = jnp.where(
                     wide == column, value, 0.0
                 ).astype(jnp.bfloat16)
@@ -377,93 +403,101 @@
             drain(f_send.at[1], blocks_ref)
             kinetic([speed_ref[pl.ds(8 * c, 8), :] for c in range(3)], t - 2)
 
-        index = [[ids[pl.ds(16 * side + 8 * h, 8), :] for h in range(2)] for side in range(2)]
-        low = [[index[s][h] & 127 for h in range(2)] for s in range(2)]
-        for r in range(24):
-            source = jnp.broadcast_to(cur[pl.ds(r, 1), :], (8, 128))
-            for s in range(2):
-                for h in range(2):
-                    pair_x[s, h, r] = pick(source, low[s][h])
-
-        in_home = [[index[s][h] < 128 for h in range(2)] for s in range(2)]
-        in_x = [[index[s][h] < 256 for h in range(2)] for s in range(2)]
+        index = [[ids[pl.ds(24 * side + 8 * p, 8), :] for p in range(3)] for side in range(2)]
+        low = [[x & 127 for x in side] for side in index]
+
+        def gather(row, keep, places, which):
+            for side, p, k in which:
+                width = PASSES[p][1]
+                for c in range(3):
+                    if side == 0:
+                        source = rows_of(lambda n: row(c, n), width, k)
+                    else:
+                        source = jnp.broadcast_to(row(c, k), (8, 128))
+                    slot = where_is(side, p, c, k)
+                    value = pick(source, places[side][p][c])
+                    if keep is not None:
+                        value = jnp.where(keep[side][p], pair_x[slot], value)
+                    pair_x[slot] = value
+
+        def blocks_of(passes):
+            return [(1, p, k) for k in range(8) for p in passes] + [
+                (0, p, k) for p in passes for k in range(PASSES[p][1])
+            ]
+
+        everywhere = [[[x] * 3 for x in side] for side in low]
+        gather(lambda c, k: cur[pl.ds(8 * c + k, 1), :], None, everywhere, blocks_of(range(3)))
+
+        in_home = [[x < 128 for x in side] for side in index]
+        in_x = [[x < 256 for x in side] for side in index]
+        in_near = [[x < 256 + FIRST for x in side] for side in index]
+        near_place, far_place = [
+            [[[(x + width * c) & 127 for c in range(3)] for x in side] for side in low]
+            for width in (FIRST, SECOND)
+        ]
         copies[0].wait_recv()
-        for r in range(24):
-            source = jnp.broadcast_to(got_x[pl.ds(r, 1), :], (8, 128))
-            for s in range(2):
-                for h in range(2):
-                    pair_x[s, h, r] = jnp.where(
-                        in_home[s][h], pair_x[s, h, r], pick(source, low[s][h])
-                    )
+        gather(lambda c, k: got_x[pl.ds(8 * c + k, 1), :], in_home, everywhere, blocks_of(range(3)))
 
         drain(c_recv.at[1], blocks_ref.at[pl.ds(0, 2)])
-        in_near = [[index[s][h] < 256 + FIRST for h in range(2)] for s in range(2)]
-
-        def places(width):
-            return [[[(low[s][h] + width * c) & 127 for c in range(3)] for h in range(2)] for s in range(2)]
-
-        near_place, far_place = places(FIRST), places(SECOND)
         near[pl.ds(0, 8), :] = merge(packed[0], [got_m[n] for n in range(2)])
-        for k in range(8):
-            source = jnp.broadcast_to(near[pl.ds(k, 1), :], (8, 128))
-            for c in range(3):
-                for s in range(2):
-                    for h in range(2):
-                        pair_x[s, h, 8 * c + k] = jnp.where(
-                            in_x[s][h],
-                            pair_x[s, h, 8 * c + k],
-                            pick(source, near_place[s][h][c]),
-                        )
+        gather(lambda c, k: near[pl.ds(k, 1), :], in_x, near_place, blocks_of(range(3)))
 
         drain(c_recv.at[2], blocks_ref.at[pl.ds(0, 4)])
         near[pl.ds(8, 8), :] = merge(packed[1], [got_m[n] for n in range(2, 6)])
 
-        def complete(k, h):
-            source = jnp.broadcast_to(near[pl.ds(8 + k, 1), :], (8, 128))
-            for c in range(3):
-                for s in range(2):
-                    pair_x[s, h, 8 * c + k] = jnp.where(
-                        in_near[s][h],
-                        pair_x[s, h, 8 * c + k],
-                        pick(source, far_place[s][h][c]),
-                    )
-
-        for k in range(8):
-            complete(k, 0)
+        def complete(which):
+            gather(lambda c, k: near[pl.ds(8 + k, 1), :], in_near, far_place, which)
+
+        complete(blocks_of(range(1)))
 
         energy = jnp.zeros((8, 128), F32)
+        sublane = lax.broadcasted_iota(jnp.int32, (8, 128), 0)
         lefts = []
         parts = []
-        for h in range(2):
-            usable = jnp.where(index[0][h] == CL_PAD, 0.0, 1.0)
-            distinct = jnp.where(index[0][h] == index[1][h], 0.0, usable)
+        for p, (begin, width) in enumerate(PASSES):
+            usable = jnp.where(index[0][p] == CL_PAD, 0.0, 1.0)
+            distinct = jnp.where(index[0][p] == index[1][p], 0.0, usable)
+            limits = [distinct]
+            for n in range(1, 8 // width):
+                limits.append(jnp.where(sublane < n * width, usable, distinct))
+            limits.append(usable)
             second = [[None] * 3 for _ in range(8)]
-            for k in range(8):
-                xi = [pair_x[0, h, 8 * c + k] for c in range(3)]
+            for k in range(width):
+                xi = [pair_x[where_is(0, p, c, k)] for c in range(3)]
                 first = [None] * 3
                 for l in range(8):
-                    d = [xi[c] - pair_x[1, h, 8 * c + l] for c in range(3)]
-                    u = jnp.maximum((usable if k < l else distinct) - dot3(d, d), 0.0)
+                    limit = limits[min(max(-((k - l) // width), 0), 8 // width)]
+                    d = [xi[c] - pair_x[where_is(1, p, c, l)] for c in range(3)]
+                    u = jnp.maximum(limit - dot3(d, d), 0.0)
                     uu = u * u
                     energy = energy + uu * u
                     for c in range(3):
                         push = uu * d[c]
                         first[c] = push if l == 0 else first[c] + push
                         second[l][c] = push if k == 0 else second[l][c] + push
-                for c in range(3):
-                    pair_f[pl.ds((8 * c + k) * PITCH + 8 * h, 8), :] = first[c]
-                if h == 0:
-                    complete(k, 1)
+                for n in range(8 // width):
+                    for c in range(3):
+                        pair_f[pl.ds((8 * c + k + n * width) * PITCH + begin, width), :] = roll(
+                            first[c], -n * width, 0
+                        )[:width]
+                if p == 0:
+                    complete(
+                        [(1, 1, k), (1, 2, k)]
+                        + ([(0, 1, k)] if k < 4 else [(0, 2, k - 4)] if k < 6 else [])
+                    )
             for l in range(8):
                 for c in range(3):
-                    pair_f[pl.ds((24 + 8 * c + l) * PITCH + 8 * h, 8), :] = second[l][c]
-
-            groups = range(8) if h == 0 else range(8, GROUPS)
+                    value = second[l][c]
+                    turn = 4
+                    while turn >= width:
+                        value = value + roll(value, turn, 0)
+                        turn //= 2
+                    pair_f[pl.ds((24 + 8 * c + l) * PITCH + begin, width), :] = value[:width]
             left = jnp.concatenate(
                 [
                     halves(pair_f[pl.ds(24 * PITCH * side + g, 24, stride=PITCH), :])
                     for side in range(2)
-                    for g in groups
+                    for g in range(begin, begin + width)
                 ],
                 axis=1,
             )
@@ -471,12 +505,15 @@
             parts.append(
                 jnp.dot(
                     left,
-                    table[pl.ds(2048 * h, left.shape[1]), pl.ds(128 if h == 0 else 256, 256 if h == 0 else 128)],
+                    table[
+                        pl.ds(256 * begin, left.shape[1]),
+                        pl.ds(128 if p == 0 else 256, 256 if p == 0 else 128),
+                    ],
                     preferred_element_type=F32,
                 )
             )
 
-        halo = parts[0][:, 128:] + parts[1]
+        halo = parts[0][:, 128:] + parts[1] + parts[2]
         halo = halo[:24] + halo[24:]
         returns = force_copies()
         beyond = [halo[8 * c : 8 * c + 8] for c in range(3)]
@@ -487,8 +524,8 @@
         for number in NEAR:
             returns[number].start()
         rest = jnp.dot(
-            lefts[1],
-            table[pl.ds(2048, lefts[1].shape[1]), pl.ds(0, 256)],
+            jnp.concatenate(lefts[1:], axis=1),
+            table[pl.ds(2048, 1536), pl.ds(0, 256)],
             preferred_element_type=F32,
         )
         halo = parts[0][:, :128] + rest[:, 128:]
@@ -579,10 +616,13 @@
         ).start()
 
     def total_of(slots):
-        total = slots[0]
-        for n in range(1, slots.shape[0]):
-            total = total + slots[n]
-        return total
+        terms = [slots[n] for n in range(slots.shape[0])]
+        while len(terms) > 1:
+            terms = [
+                terms[n] + terms[n + 1] if n + 1 < len(terms) else terms[n]
+                for n in range(0, len(terms), 2)
+            ]
+        return terms[0]
 
     offsets = [(0, y, z) for y in range(sizes[1]) for z in range(sizes[2]) if y or z]
     own = me[1] * sizes[2] + me[2]
@@ -655,7 +695,7 @@
             vmem((24, 128), F32),
             vmem((24, 128), F32),
             vmem((8, 128), F32),
-            vmem((32, 128), jnp.int32),
+            vmem((48, 128), jnp.int32),
             vmem((8, 128), jnp.int32),
             vmem((8, 128), F32),
             vmem((2 * SLOTS, 384), jnp.bfloat16),
@@ -663,7 +703,7 @@
             vmem((256, 384), jnp.bfloat16),
             vmem((16, 128), F32),
             vmem((24 + 8 * (2 * NORDER + 1), 128), F32),
-            vmem((2, 2, 24, 8, 128), F32),
+            vmem((114, 8, 128), F32),
             vmem((48 * PITCH, 128), F32),
             vmem((24, 128), F32),
             vmem((2, 8, 128), F32),

time: 92.8 us -> 92.6 us (level)
  no operation moved by 1% of the time
where the time goes in v8:
time: 92.6 us; the launch traced here: 92.4 us
  Pallas kernels  91.8 us (99%)
    pallas_call x1, Pallas kernels, on_device(): pl.pallas_call(functools.partial(kernel, sizes), out_shape=(jax.ShapeDtyp...  91.1 us

profile of v8, /device:TPU:65, one launch (start us, length us, event | category | flops | bytes accessed | tf_op | source)
XLA Modules:
  0.0 92.4 jit_solution(127961528441645214)
XLA Ops:
  0.6 91.1 %membrane.1 = (f32[3,8,128]{2,1,0:T(8,128)S(1)}, f32[3,8,128]{2,1,0:T(8,128)S(1)}, f32[1,128]{1,0:T(1,128)S(1)}) custom-call(f32[3,8,128]{2,1,0:T(8,128)} %pos_in.1, f32[3,8,128]{2,1,0:T(8,128)} %vel_in.1, s32[1,178]{1,0:T(1,128)} %bitcast.2, s32[2,1792]{1,0:T(2,128)} %pair_in.1, s32[7,128]{1,0:T(8,128)} %flag_in.1), custom_call_target="tpu_custom_call" | custom-call | tf_op jit(solution)/shard_map/membrane/pallas_call | solution.py:685
  91.8 0.7 finish.1

commit v9 on v8

--- a/solution.py
+++ b/solution.py
@@ -428,19 +428,19 @@
         everywhere = [[[x] * 3 for x in side] for side in low]
         gather(lambda c, k: cur[pl.ds(8 * c + k, 1), :], None, everywhere, blocks_of(range(3)))
 
-        in_home = [[x < 128 for x in side] for side in index]
+        not_x = [[(x < 128) | (x >= 256) for x in side] for side in index]
         in_x = [[x < 256 for x in side] for side in index]
         in_near = [[x < 256 + FIRST for x in side] for side in index]
         near_place, far_place = [
             [[[(x + width * c) & 127 for c in range(3)] for x in side] for side in low]
             for width in (FIRST, SECOND)
         ]
-        copies[0].wait_recv()
-        gather(lambda c, k: got_x[pl.ds(8 * c + k, 1), :], in_home, everywhere, blocks_of(range(3)))
-
         drain(c_recv.at[1], blocks_ref.at[pl.ds(0, 2)])
         near[pl.ds(0, 8), :] = merge(packed[0], [got_m[n] for n in range(2)])
         gather(lambda c, k: near[pl.ds(k, 1), :], in_x, near_place, blocks_of(range(3)))
+
+        copies[0].wait_recv()
+        gather(lambda c, k: got_x[pl.ds(8 * c + k, 1), :], not_x, everywhere, blocks_of(range(3)))
 
         drain(c_recv.at[2], blocks_ref.at[pl.ds(0, 4)])
         near[pl.ds(8, 8), :] = merge(packed[1], [got_m[n] for n in range(2, 6)])

time: 92.6 us -> 92.6 us (level)
  no operation moved by 1% of the time
where the time goes in v9:
time: 92.6 us; the launch traced here: 92.5 us
  Pallas kernels  91.8 us (99%)
    pallas_call x1, Pallas kernels, on_device(): pl.pallas_call(functools.partial(kernel, sizes), out_shape=(jax.ShapeDtyp...  91.2 us

profile of v9, /device:TPU:65, one launch (start us, length us, event | category | flops | bytes accessed | tf_op | source)
XLA Modules:
  0.0 92.5 jit_solution(15995068383795115629)
XLA Ops:
  0.6 91.2 %membrane.1 = (f32[3,8,128]{2,1,0:T(8,128)S(1)}, f32[3,8,128]{2,1,0:T(8,128)S(1)}, f32[1,128]{1,0:T(1,128)S(1)}) custom-call(f32[3,8,128]{2,1,0:T(8,128)} %pos_in.1, f32[3,8,128]{2,1,0:T(8,128)} %vel_in.1, s32[1,178]{1,0:T(1,128)} %bitcast.2, s32[2,1792]{1,0:T(2,128)} %pair_in.1, s32[7,128]{1,0:T(8,128)} %flag_in.1), custom_call_target="tpu_custom_call" | custom-call | tf_op jit(solution)/shard_map/membrane/pallas_call | solution.py:685
  91.8 0.7 finish.1

commit v10 on v9

--- a/solution.py
+++ b/solution.py
@@ -704,7 +704,7 @@
             vmem((16, 128), F32),
             vmem((24 + 8 * (2 * NORDER + 1), 128), F32),
             vmem((114, 8, 128), F32),
-            vmem((48 * PITCH, 128), F32),
+            vmem((49 * PITCH, 128), F32),
             vmem((24, 128), F32),
             vmem((2, 8, 128), F32),
             vmem((24, 128), F32),

time: 92.6 us -> 92.6 us (level)
  no operation moved by 1% of the time
where the time goes in v10:
time: 92.6 us; the launch traced here: 92.5 us
  Pallas kernels  91.8 us (99%)
    pallas_call x1, Pallas kernels, on_device(): pl.pallas_call(functools.partial(kernel, sizes), out_shape=(jax.ShapeDtyp...  91.2 us

profile of v10, /device:TPU:65, one launch (start us, length us, event | category | flops | bytes accessed | tf_op | source)
XLA Modules:
  0.0 92.5 jit_solution(14104552521880470539)
XLA Ops:
  0.6 91.2 %membrane.1 = (f32[3,8,128]{2,1,0:T(8,128)S(1)}, f32[3,8,128]{2,1,0:T(8,128)S(1)}, f32[1,128]{1,0:T(1,128)S(1)}) custom-call(f32[3,8,128]{2,1,0:T(8,128)} %pos_in.1, f32[3,8,128]{2,1,0:T(8,128)} %vel_in.1, s32[1,178]{1,0:T(1,128)} %bitcast.2, s32[2,1792]{1,0:T(2,128)} %pair_in.1, s32[7,128]{1,0:T(8,128)} %flag_in.1), custom_call_target="tpu_custom_call" | custom-call | tf_op jit(solution)/shard_map/membrane/pallas_call | solution.py:685
  91.8 0.7 finish.1

commit v11 on v10

--- a/solution.py
+++ b/solution.py
@@ -135,9 +135,8 @@
     return direction, expansion(coupling)
 
 
-def constrain(updated, direction, weights, rest, flags):
-    links = [x - up(x) for x in updated]
-    solution = expand(weights, flags * root_half * (dot3(direction, links) - rest))
+def constrain(updated, links, source, direction, weights, rest, flags):
+    solution = expand(weights, source)
     shifts = [x * (root_half * solution) for x in direction]
     updated = [x - s + down(s) for x, s in zip(updated, shifts)]
     links = [x - (s + s) + (down(s) + up(s)) for x, s in zip(links, shifts)]
@@ -563,24 +562,32 @@
         own = [
             own[8 * c : 8 * c + 8] + came[:, 128 * c : 128 * c + 128] for c in range(3)
         ]
+        again = jnp.where(t > 0, 1.0, 0.0).astype(F32)
+        share = F32(0.5 * time_step)
+        gain = share * F32(time_step) * (1.0 + again)
+        calm = [half_ref[pl.ds(8 * c, 8), :] + again * (share * own[c]) for c in range(3)]
+        base = [
+            cur[pl.ds(8 * c, 8), :] + time_step * (calm[c] + share * own[c]) for c in range(3)
+        ]
+        base_links = [x - up(x) for x in base]
+        held = flag8[...] * root_half
+        source = held * (dot3(direction, base_links) - rest_ref[...])
+        pull = [held * gain * d for d in direction]
         drain(f_recv.at[2], blocks_ref.at[pl.ds(0, 4)])
         came = merge(packed[1], [ret_m[n] for n in range(2, 6)])
         came = jnp.dot(halves(came), back2[pl.ds(128, 128), :], preferred_element_type=F32)
         came = came[:8] + came[8:]
-        force = [
-            0.5 * time_step * (own[c] + came[:, 128 * c : 128 * c + 128])
-            for c in range(3)
-        ]
-
-        again = jnp.where(t > 0, 1.0, 0.0).astype(F32)
-        speed = [half_ref[pl.ds(8 * c, 8), :] + again * force[c] for c in range(3)]
+        came = [came[:, 128 * c : 128 * c + 128] for c in range(3)]
+        speed = [calm[c] + (again * share) * came[c] for c in range(3)]
 
         @pl.when(t < ITERS)
         def _():
-            half = [speed[c] + force[c] for c in range(3)]
             before = [cur[pl.ds(8 * c, 8), :] for c in range(3)]
+            bends = [x - up(x) for x in came]
             moved = constrain(
-                [x + time_step * v for x, v in zip(before, half)],
+                [x + gain * f for x, f in zip(base, came)],
+                [x + gain * b for x, b in zip(base_links, bends)],
+                source + dot3(pull, bends),
                 [frame[pl.ds(8 * n, 8), :] for n in range(3)],
                 [frame[pl.ds(8 * n, 8), :] for n in range(3, 3 + 2 * NORDER + 1)],
                 rest_ref[...],

time: 92.6 us -> 92.6 us (level)
  no operation moved by 1% of the time
where the time goes in v11:
time: 92.6 us; the launch traced here: 92.5 us
  Pallas kernels  91.8 us (99%)
    pallas_call x1, Pallas kernels, on_device(): pl.pallas_call(functools.partial(kernel, sizes), out_shape=(jax.ShapeDtyp...  91.2 us

profile of v11, /device:TPU:65, one launch (start us, length us, event | category | flops | bytes accessed | tf_op | source)
XLA Modules:
  0.0 92.5 jit_solution(7362629771427267968)
XLA Ops:
  0.6 91.2 %membrane.1 = (f32[3,8,128]{2,1,0:T(8,128)S(1)}, f32[3,8,128]{2,1,0:T(8,128)S(1)}, f32[1,128]{1,0:T(1,128)S(1)}) custom-call(f32[3,8,128]{2,1,0:T(8,128)} %pos_in.1, f32[3,8,128]{2,1,0:T(8,128)} %vel_in.1, s32[1,178]{1,0:T(1,128)} %bitcast.2, s32[2,1792]{1,0:T(2,128)} %pair_in.1, s32[7,128]{1,0:T(8,128)} %flag_in.1), custom_call_target="tpu_custom_call" | custom-call | tf_op jit(solution)/shard_map/membrane/pallas_call | solution.py:692
  91.8 0.7 finish.1

commit v12 on v10

--- a/solution.py
+++ b/solution.py
@@ -305,7 +305,7 @@
                 pltpu.make_async_remote_copy(
                     src_ref=source,
                     dst_ref=target,
-                    send_sem=c_send.at[0 if number == 0 else 1],
+                    send_sem=c_send.at[0],
                     recv_sem=c_recv.at[0 if number == 0 else 1 if number in NEAR else 2],
                     device_id=at(tuple(-z for z in zone)),
                     device_id_type=MESH,
@@ -322,7 +322,7 @@
                 pltpu.make_async_remote_copy(
                     src_ref=source,
                     dst_ref=target,
-                    send_sem=f_send.at[0 if number == 0 else 1],
+                    send_sem=f_send.at[0],
                     recv_sem=f_recv.at[0 if number == 0 else 1 if number in NEAR else 2],
                     device_id=at(zone),
                     device_id_type=MESH,
@@ -399,8 +399,7 @@
         def _():
             pl.when(t > 1)(hear)
             tell()
-            force_copies()[0].wait_send()
-            drain(f_send.at[1], blocks_ref)
+            drain(f_send.at[0], blocks_ref)
             kinetic([speed_ref[pl.ds(8 * c, 8), :] for c in range(3)], t - 2)
 
         index = [[ids[pl.ds(24 * side + 8 * p, 8), :] for p in range(3)] for side in range(2)]
@@ -549,8 +548,7 @@
         for n, value in enumerate(direction + weights):
             frame[pl.ds(8 * n, 8), :] = value
 
-        copies[0].wait_send()
-        drain(c_send.at[1], blocks_ref)
+        drain(c_send.at[0], blocks_ref)
         returns[0].wait_recv()
         came = jnp.dot(
             halves(ret_x[...]), back[...], preferred_element_type=F32
@@ -631,8 +629,7 @@
     plane[own] = row[...]
     hear()
     tell()
-    force_copies()[0].wait_send()
-    drain(f_send.at[1], blocks_ref)
+    drain(f_send.at[0], blocks_ref)
     hear()
     drain(p_recv.at[0], rows_ref.at[pl.ds(0, len(offsets))])
     mid[...] = total_of(plane)
@@ -643,7 +640,7 @@
     def _():
         for x, _, _ in offsets:
             for z in range(sizes[2]):
-                copy_row(mid, line.at[me[0]], (x, 0, z), l_send.at[z], l_recv.at[0])
+                copy_row(mid, line.at[me[0]], (x, 0, z), l_send.at[0], l_recv.at[0])
 
     line[me[0]] = mid[...]
     drain(p_send.at[0], rows_ref.at[pl.ds(0, plane.shape[0] - 1)])
@@ -652,8 +649,7 @@
 
     @pl.when(lead)
     def _():
-        for z in range(sizes[2]):
-            drain(l_send.at[z], rows_ref.at[pl.ds(0, len(offsets))])
+        drain(l_send.at[0], rows_ref.at[pl.ds(0, sizes[2] * len(offsets))])
 
 
 CL_PAD = 306
@@ -717,13 +713,13 @@
             vmem((plane, 1, 128), F32),
             vmem((1, 128), F32),
             vmem((sizes[0], 1, 128), F32),
-            dma((2,)),
+            dma((1,)),
             dma((3,)),
-            dma((2,)),
+            dma((1,)),
             dma((3,)),
             dma((1,)),
             dma((1,)),
-            dma((sizes[2],)),
+            dma((1,)),
             dma((1,)),
             pltpu.SemaphoreType.REGULAR((4,)),
             vmem((3, 8, 128), F32),
@@ -732,8 +728,8 @@
             vmem((2, SLOTS), jnp.int32),
             vmem((7, 128), jnp.int32),
             dma((5,)),
-            vmem((6, 8, 128), F32),
-            vmem((max(plane, sizes[0]) - 1, 1, 128), F32),
+            vmem((9, 8, 128), F32),
+            vmem((max(plane - 1, sizes[2] * (sizes[0] - 1)), 1, 128), F32),
             vmem((24, 128), F32),
             vmem((4, 8, 128), jnp.int32),
             vmem((2, 8, 128), F32),

time: 92.6 us -> 92.6 us (level)
  no operation moved by 1% of the time
where the time goes in v12:
time: 92.6 us; the launch traced here: 92.4 us
  Pallas kernels  91.8 us (99%)
    pallas_call x1, Pallas kernels, on_device(): pl.pallas_call(functools.partial(kernel, sizes), out_shape=(jax.ShapeDtyp...  91.1 us

profile of v12, /device:TPU:65, one launch (start us, length us, event | category | flops | bytes accessed | tf_op | source)
XLA Modules:
  0.0 92.4 jit_solution(511119347887828889)
XLA Ops:
  0.6 91.1 %membrane.1 = (f32[3,8,128]{2,1,0:T(8,128)S(1)}, f32[3,8,128]{2,1,0:T(8,128)S(1)}, f32[1,128]{1,0:T(1,128)S(1)}) custom-call(f32[3,8,128]{2,1,0:T(8,128)} %pos_in.1, f32[3,8,128]{2,1,0:T(8,128)} %vel_in.1, s32[1,178]{1,0:T(1,128)} %bitcast.2, s32[2,1792]{1,0:T(2,128)} %pair_in.1, s32[7,128]{1,0:T(8,128)} %flag_in.1), custom_call_target="tpu_custom_call" | custom-call | tf_op jit(solution)/shard_map/membrane/pallas_call | solution.py:681
  91.8 0.7 finish.1
